TPU v7x, 32 devices: a whole 2x2x4 slice. The times are simulated.
32 devices in a mesh: ens: 2 (over x), slab: 4 (over z), feat: 4 (over y, core).
Axes of the slice: x: 2, y: 2, z: 4, core: 2. Of those that a mesh axis runs over, the one named last changes fastest.
Arguments:
- particles: float32 [3072, 14336], P('ens', ('slab', 'feat')), parts along dimension 0
- prec_diag: float32 [28672], P(('ens', 'slab', 'feat')), parts along dimension 0
- mean_vec: float32 [28672], P(('ens', 'slab', 'feat')), parts along dimension 0
- low_rank: bfloat16 [28672, 16], P(('ens', 'slab', 'feat')), parts along dimension 0
Outputs:
- output: float32 [3072, 14336], P('ens', ('slab', 'feat')), parts along dimension 0
There are 2 independent parts. A program takes and returns all parts, laid end to end along the dimension named above; each array names one.
All inputs are finite; a program needn't handle non-finite values.
Results may differ from a plain program's by a relative error of at most 0.001.
Values are sent between devices in bfloat16 or wider.
A program may use at most 1 GiB of HBM per device.

v0:
```python
import jax
import jax.numpy as jnp
from jax import lax
from jax.sharding import PartitionSpec as P

NUM_STEPS = 3
BAND_SCALE = 4.0
STEP_SCALE = 0.4
FEAT_AXES = ("slab", "feat")
LEAD_AXES = ("ens", "slab", "feat")


def solution(mesh):
    def run_steps(particles, prec_diag, mean_vec, low_rank):
        total_rows, width = particles.shape
        n_part = total_rows // mesh.shape["ens"]
        bandwidth = BAND_SCALE * width
        step_size = STEP_SCALE * width
        rep_coef = 2.0 / bandwidth

        def local_steps(current, prec_loc, mean_loc, fac_loc):
            for step_index in range(NUM_STEPS):
                centered = current - mean_loc[None, :]
                proj_part = jnp.dot(centered.astype(jnp.bfloat16), fac_loc, preferred_element_type=jnp.float32)
                proj_full = lax.psum(proj_part, FEAT_AXES)
                cur_bf = current.astype(jnp.bfloat16)
                gram_part = jnp.einsum("nd,md->nm", cur_bf, cur_bf, preferred_element_type=jnp.float32)
                gram_full = lax.psum(gram_part, FEAT_AXES)
                low_term = jnp.einsum("nr,dr->nd", proj_full.astype(jnp.bfloat16), fac_loc, preferred_element_type=jnp.float32)
                grad_log = -(centered * prec_loc[None, :] + low_term)
                gram_diag = jnp.diagonal(gram_full)
                sq_dist = jnp.maximum(gram_diag[:, None] + gram_diag[None, :] - 2.0 * gram_full, 0.0)
                kernel = jnp.exp(-sq_dist / bandwidth)
                drive_term = grad_log - rep_coef * current
                applied = jnp.dot(kernel.astype(jnp.bfloat16), drive_term.astype(jnp.bfloat16), preferred_element_type=jnp.float32)
                phi_dir = (applied + rep_coef * jnp.sum(kernel, axis=1)[:, None] * current) / n_part
                current = current + step_size * phi_dir
            return current

        sharded = jax.shard_map(
            local_steps,
            mesh=mesh,
            in_specs=(P("ens", FEAT_AXES), P(LEAD_AXES), P(LEAD_AXES), P(LEAD_AXES, None)),
            out_specs=P("ens", FEAT_AXES),
            check_vma=False,
        )
        return sharded(particles, prec_diag, mean_vec, low_rank)

    return run_steps
```

profile of v0, /device:TPU:0, one launch (start us, length us, event | category | flops | bytes accessed | tf_op | source)
XLA Modules:
  0.0 774.2 jit_solution(9869854138696471393)
XLA Ops:
  6.5 0.0 copy-start
  6.5 0.0 all-reduce.4.cloned.1.call-start
  6.5 11.7 %fusion.52 = f32[1536,1536]{1,0:T(8,128)} fusion(f32[1536,896]{1,0:T(8,128)} %param.4), kind=kOutput, calls=%fused_computation.58 | convolution fusion | flops 4229234688 | bytes 14942208 | tf_op jit(solution)/shard_map/nd,md->nm/dot_general | solution.py:27
  18.3 0.0 all-reduce.4.cloned.1.call-update
  18.3 0.0 all-reduce.6.cloned.1.call-start
  18.4 0.0 copy-done
  18.4 0.6 copy-done.1
  19.0 3.4 fusion.33
  22.4 84.0 %psum.43 = bf16[1536,16]{1,0:T(8,128)(2,1)S(1)} all-reduce(f32[1536,16]{1,0:T(8,128)S(1)} %fusion.33), channel_id=1, replica_groups=mesh['ens'=2,'slab'=4,'feat'=4] {'slab','feat'}, use_global_device_ids=true, to_apply=%region_1.0 | all-reduce | flops 24576 | bytes 147456 | tf_op jit(solution)/shard_map/psum | solution.py:25
  106.4 107.3 %all-reduce.4.cloned.1.call-done = f32[1536,1536]{1,0:T(8,128)} async-done(((f32[1536,1536]{1,0:T(8,128)}), f32[1536,1536]{1,0:T(8,128)}) %all-reduce.4.cloned.1.call-update) | async-done | bytes 9437200 | tf_op jit(solution)/shard_map/psum | solution.py:28
  213.7 26.0 %gather_fusion = f32[1536]{0:T(1024)S(1)} fusion(f32[1536,1536]{1,0:T(8,128)} %all-reduce.4.cloned.1.call-done, s32[1536]{0:T(1024)S(1)} %or_reduce_fusion), kind=kCustom, calls=%fused_computation | custom fusion | bytes 24576 | tf_op jit(solution)/shard_map/jit(diagonal)/cond/branch_0_fun/gather | solution.py:31
  239.7 0.0 copy-start.2
  239.7 5.4 fusion
  245.1 0.0 copy-done.2
  245.1 16.7 %multiply_add_fusion.2 = f32[1536,896]{1,0:T(8,128)} fusion(f32[1536,896]{1,0:T(8,128)} %param.4, f32[1536,1536]{1,0:T(8,128)} %all-reduce.4.cloned.1.call-done, f32[1536]{0:T(1024)S(1)} %gather_fusion, bf16[896,16]{0,1:T(8,128)(2,1)S(1)} %copy-done, f32[1536]{0:T(1024)S(1)} %broadcast_multiply_fusion.2, f32[896]{0:T(1024)S(1)} %copy-done.2, ...), kind=kOutput, calls=%fused_computation.16 | convolution fusion | flops 4303552512 | bytes 20544512 | tf_op jit(solution)/shard_map/dot_general | solution.py:35
  261.9 11.7 %fusion.38 = f32[1536,1536]{1,0:T(8,128)} fusion(f32[1536,896]{1,0:T(8,128)} %multiply_add_fusion.2), kind=kOutput, calls=%fused_computation.44 | convolution fusion | flops 4229234688 | bytes 14942208 | tf_op jit(solution)/shard_map/nd,md->nm/dot_general | solution.py:27
  273.6 0.0 all-reduce.6.cloned.1.call-update
  273.6 0.0 all-reduce.8.cloned.1.call-start
  273.7 3.4 fusion.34
  277.1 81.6 %psum.45 = bf16[1536,16]{1,0:T(8,128)(2,1)S(1)} all-reduce(f32[1536,16]{1,0:T(8,128)S(1)} %fusion.34), channel_id=1, replica_groups=mesh['ens'=2,'slab'=4,'feat'=4] {'slab','feat'}, use_global_device_ids=true, to_apply=%region_4.5 | all-reduce | flops 24576 | bytes 147456 | tf_op jit(solution)/shard_map/psum | solution.py:25
  358.8 107.8 %all-reduce.6.cloned.1.call-done = f32[1536,1536]{1,0:T(8,128)} async-done(((f32[1536,1536]{1,0:T(8,128)}), f32[1536,1536]{1,0:T(8,128)}) %all-reduce.6.cloned.1.call-update) | async-done | bytes 9437200 | tf_op jit(solution)/shard_map/psum | solution.py:28
  466.6 26.0 %gather_fusion.1 = f32[1536]{0:T(1024)S(1)} fusion(f32[1536,1536]{1,0:T(8,128)} %all-reduce.6.cloned.1.call-done, s32[1536]{0:T(1024)S(1)} %or_reduce_fusion), kind=kCustom, calls=%fused_computation.1 | custom fusion | bytes 24576 | tf_op jit(solution)/shard_map/jit(diagonal)/cond/branch_0_fun/gather | solution.py:31
  492.7 5.4 fusion.2
  498.1 16.9 %multiply_add_fusion.1 = f32[1536,896]{1,0:T(8,128)} fusion(f32[1536,896]{1,0:T(8,128)} %multiply_add_fusion.2, f32[1536,1536]{1,0:T(8,128)} %all-reduce.6.cloned.1.call-done, f32[1536]{0:T(1024)S(1)} %gather_fusion.1, bf16[896,16]{0,1:T(8,128)(2,1)S(1)} %copy-done, f32[1536]{0:T(1024)S(1)} %broadcast_multiply_fusion.1, f32[896]{0:T(1024)S(1)} %copy-done.2, ...), kind=kOutput, calls=%fused_computation.14 | convolution fusion | flops 4303552512 | bytes 20544512 | tf_op jit(solution)/shard_map/dot_general | solution.py:35
  514.9 11.6 %fusion.36 = f32[1536,1536]{1,0:T(8,128)} fusion(f32[1536,896]{1,0:T(8,128)} %multiply_add_fusion.1), kind=kOutput, calls=%fused_computation.42 | convolution fusion | flops 4229234688 | bytes 14942208 | tf_op jit(solution)/shard_map/nd,md->nm/dot_general | solution.py:27
  526.6 0.0 all-reduce.8.cloned.1.call-update
  526.6 3.4 fusion.35
  530.0 81.6 %psum.47 = bf16[1536,16]{1,0:T(8,128)(2,1)S(1)} all-reduce(f32[1536,16]{1,0:T(8,128)S(1)} %fusion.35), channel_id=1, replica_groups=mesh['ens'=2,'slab'=4,'feat'=4] {'slab','feat'}, use_global_device_ids=true, to_apply=%region_7.8 | all-reduce | flops 24576 | bytes 147456 | tf_op jit(solution)/shard_map/psum | solution.py:25
  611.7 107.8 %all-reduce.8.cloned.1.call-done = f32[1536,1536]{1,0:T(8,128)} async-done(((f32[1536,1536]{1,0:T(8,128)}), f32[1536,1536]{1,0:T(8,128)}) %all-reduce.8.cloned.1.call-update) | async-done | bytes 9437200 | tf_op jit(solution)/shard_map/psum | solution.py:28
  719.5 26.0 %gather_fusion.2 = f32[1536]{0:T(1024)S(1)} fusion(f32[1536,1536]{1,0:T(8,128)} %all-reduce.8.cloned.1.call-done, s32[1536]{0:T(1024)S(1)} %or_reduce_fusion), kind=kCustom, calls=%fused_computation.2 | custom fusion | bytes 24576 | tf_op jit(solution)/shard_map/jit(diagonal)/cond/branch_0_fun/gather | solution.py:31
  745.6 5.4 fusion.4
  751.0 16.7 %multiply_add_fusion = f32[1536,896]{1,0:T(8,128)} fusion(f32[1536,896]{1,0:T(8,128)} %multiply_add_fusion.1, f32[1536,1536]{1,0:T(8,128)} %all-reduce.8.cloned.1.call-done, f32[1536]{0:T(1024)S(1)} %gather_fusion.2, bf16[896,16]{0,1:T(8,128)(2,1)S(1)} %copy-done, f32[1536]{0:T(1024)S(1)} %broadcast_multiply_fusion, f32[896]{0:T(1024)S(1)} %copy-done.2, ...), kind=kOutput, calls=%fused_computation.12 | convolution fusion | flops 4303552512 | bytes 20544512 | tf_op jit(solution)/shard_map/dot_general | solution.py:35
  (5 shorter events, 0.1 us)
Async XLA Ops:
  6.5 11.9 %copy-start = (bf16[896,16]{0,1:T(8,128)(2,1)S(1)}, bf16[896,16]{0,1:T(8,128)(2,1)}, u32[]{:S(2)}) copy-start(bf16[896,16]{0,1:T(8,128)(2,1)} %param.7) | copy-start | bytes 86020
  6.5 207.1 %all-reduce.4.cloned.1.call-start = ((), (), s32[]{:S(2)}) async-start(), calls=%async_computation | async-start | bytes 18874368 | tf_op jit(solution)/shard_map/psum | solution.py:28
  18.3 0.7 copy-start.1
  18.3 448.3 %all-reduce.6.cloned.1.call-start = ((), (), s32[]{:S(2)}) async-start(), calls=%async_computation.1 | async-start | bytes 18874368 | tf_op jit(solution)/shard_map/psum | solution.py:28
  239.7 5.4 copy-start.2
  273.6 445.9 %all-reduce.8.cloned.1.call-start = ((), (), s32[]{:S(2)}) async-start(), calls=%async_computation.2 | async-start | bytes 18874368 | tf_op jit(solution)/shard_map/psum | solution.py:28
Sparse Core Ops, SparseCore 0:
  18.4 195.1 all-reduce.3
  273.8 192.8 all-reduce.5
  526.7 192.7 all-reduce.7
where the time goes:
time: 777 us; the launch traced here: 774 us
  waiting for transfers between devices  323 us (42%)
  blocking collectives  247 us (32%)
  matrix products  95.7 us (12%)
  local copies, waits for them, and re-layouts  78.7 us (10%)
  other arithmetic  16.2 us (2%)
  between operations  13.2 us (2%)
    psum x3, waiting for transfers between devices, local_steps(): gram_full = lax.psum(gram_part, FEAT_AXES)  323 us
    psum x3, blocking collectives, local_steps(): proj_full = lax.psum(proj_part, FEAT_AXES)  247 us
    gather x3, local copies, waits for them, and re-layouts, local_steps(): gram_diag = jnp.diagonal(gram_full)  78.1 us
    dot_general x3, matrix products, local_steps(): jnp.dot(kernel.astype(jnp.bfloat16), drive_term.astype(jnp.bfloat16), pre...  50.3 us
    dot_general x3, matrix products, local_steps(): jnp.einsum('nd,md->nm', cur_bf, cur_bf, preferred_element_type=jnp.float32)  35.1 us
    reduce_sum x3, other arithmetic, local_steps(): jnp.sum(kernel, axis=1)[:, None]  16.1 us
  transfers between devices with their start and end apart: 3, of which 3 were waited for; matrix products, arithmetic and copies ran while one was open for 1% of the time, Pallas kernels for 0%

commit v1 on v0

v1 whole, which is shorter than its diff:
```python
import functools

import jax
import jax.numpy as jnp
from jax import lax
from jax.experimental import pallas as pl
from jax.experimental.pallas import tpu as pltpu
from jax.sharding import PartitionSpec as P

NUM_STEPS = 3
BAND_SCALE = 4.0
STEP_SCALE = 0.4
FEAT_AXES = ("slab", "feat")
LEAD_AXES = ("ens", "slab", "feat")
MESH = pl.DeviceIdType.MESH

B = 128
NP = 12
NB = 78
ROW = 256
UP = 6
LAG = 2
END = 2
OUT1 = 2
LAG2 = 2
OUT2 = 2
DIE = 2
FIN0 = 3 * LAG + END
AG0 = FIN0 + OUT1
CH = 15
ITERS = AG0 + 3 * LAG2 + CH + OUT2 + DIE


def _block(n):
    e = lax.div(n, NB)
    i = lax.rem(n, NP)
    j = lax.rem(i + lax.div(n, NP), NP)
    return (1 - e) * i + e * NP, (1 - e) * j + e * (n - NB)


def _at(k_ref, n):
    i, j = _block(n)
    return k_ref.at[pl.ds(pl.multiple_of(i * B, B), B), pl.ds(pl.multiple_of(j * B, B), B)]


def kernel(width, x_hbm, lam_ref, mu_ref, ut_ref, o_hbm, theta, th, a_ref, kf, gsrc, gy, zrecv, yrecv, yend, pmb, pmrecv,
           dsrc, dgather, dsum, sacc, sgather, ssum, ld, od, thd_s, thd_r, pm_s, pm_r, dg_s, dg_r, sg_s, sg_r, zs, zr, ys, yr,
           ye_s, ye_r, kz_s, kz_r, kyz_s, kyz_r, ky_s, ky_r, kd_s, kd_r, ke_s, ke_r):
    nf = theta.shape[1]
    n_part = theta.shape[0]
    bandwidth = BAND_SCALE * width
    step_size = STEP_SCALE * width
    rep = 2.0 / bandwidth
    ens = lax.axis_index("ens")
    z = lax.axis_index("slab")
    feat = lax.axis_index("feat")
    y = lax.div(feat, 2)
    c = lax.rem(feat, 2)
    me = z * 4 + feat
    ypart = (ens, z, (1 - y) * 2 + c)
    dpart = (ens, z, y * 2 + 1 - c)
    dc = lax.div(z, 3)
    corner = lax.rem(z, 3) == 0
    own8 = (dc * 2 + y) * 2 + c

    def rcopy(src, dst, s, r, dev):
        return pltpu.make_async_remote_copy(src_ref=src, dst_ref=dst, send_sem=s, recv_sem=r, device_id=dev, device_id_type=MESH)

    def zdev(dz):
        return (ens, z + dz, feat)

    def slot_chain(i, d, yy, cc):
        w = lax.div(i, 10)
        zf = lax.div(i, 2) * 16 + d * 4 + lax.rem(i, 2) * 2
        yf = (i - 10) * 16 + 8 + d * 4 + yy * 2
        return lax.rem((1 - w) * zf + w * yf + cc + NB, 80)

    def slot_yf(k, d, yy, cc):
        return lax.rem(k * 16 + 8 + d * 4 + yy * 2 + cc + NB, 80)

    def load_copy(p):
        rows = pl.ds(pl.multiple_of(p * ROW, ROW), ROW)
        return pltpu.make_async_copy(x_hbm.at[rows], theta.at[rows], ld.at[p])

    def out_copy(p):
        rows = pl.ds(pl.multiple_of(p * ROW, ROW), ROW)
        return pltpu.make_async_copy(theta.at[rows], o_hbm.at[rows], od.at[p])

    def th_copy(p):
        rows = pl.ds(pl.multiple_of(p * ROW, ROW), ROW)
        return rcopy(th.at[rows, pl.ds(0, nf)], th.at[rows, pl.ds(nf, nf)], thd_s.at[p], thd_r.at[p], dpart)

    def pm_copy():
        return rcopy(pmb.at[1 - c], pmrecv, pm_s, pm_r, dpart)

    def dg_copy(e):
        dev = (ens, (e // 4) * 3, e % 4)
        return rcopy(dsrc, dgather.at[me], dg_s.at[e], dg_r.at[me], dev)

    def dg_local():
        return pltpu.make_async_copy(dsrc, dgather.at[me], dg_r.at[me])

    def sg_copy(e):
        dev = (ens, e // 4, e % 4)
        return rcopy(sacc, sgather.at[own8], sg_s.at[e], sg_r.at[own8], dev)

    def sg_local():
        return pltpu.make_async_copy(sacc, sgather.at[own8], sg_r.at[own8])

    def z_copy(d, i):
        return rcopy(gsrc.at[d, i], zrecv.at[d, i], zs.at[d, i], zr.at[d, i], zdev(2 * d - 1))

    def y_copy(d, k):
        return rcopy(gy.at[d, k], yrecv.at[d, k], ys.at[d, k], yr.at[d, k], ypart)

    def ye_copy(k, i):
        return rcopy(gsrc.at[dc, i], yend.at[k], ye_s.at[k], ye_r.at[k], ypart)

    def kz_copy(d, i):
        blk = _at(kf, slot_chain(i, d, y, c))
        return rcopy(blk, blk, kz_s.at[d, i], kz_r.at[d, i], zdev(1 - 2 * d))

    def kyz_copy(k, ey):
        blk = _at(kf, lax.rem(k * 16 + dc * 4 + ey * 2 + c + NB, 80))
        return rcopy(blk, blk, kyz_s.at[k], kyz_r.at[k], ypart)

    def ky_copy(d, k, yy):
        blk = _at(kf, slot_yf(k, d, yy, c))
        return rcopy(blk, blk, ky_s.at[d, k], ky_r.at[d, k], ypart)

    def kd_copy(d, i, cc):
        blk = _at(kf, slot_chain(i, d, y, cc))
        return rcopy(blk, blk, kd_s.at[d, i], kd_r.at[d, i], dpart)

    def ke_copy(d, k, cc):
        blk = _at(kf, slot_yf(k, d, 1 - y, cc))
        return rcopy(blk, blk, ke_s.at[d, k], ke_r.at[d, k], dpart)

    def flip(n):
        i, j = _block(n)

        @pl.when((n >= NP) & (n < NB))
        def _():
            src = kf[pl.ds(pl.multiple_of(i * B, B), B), pl.ds(pl.multiple_of(j * B, B), B)]
            kf[pl.ds(pl.multiple_of(j * B, B), B), pl.ds(pl.multiple_of(i * B, B), B)] = (
                src.astype(jnp.float32).T.astype(jnp.bfloat16)
            )

    def gram(n):
        i, j = _block(n)
        return lax.dot_general(
            th[pl.ds(pl.multiple_of(i * B, B), B), :],
            th[pl.ds(pl.multiple_of(j * B, B), B), :],
            (((1,), (1,)), ((), ())),
            preferred_element_type=jnp.float32,
        )

    def post(p, new):
        rows = pl.ds(pl.multiple_of(p * ROW, ROW), ROW)
        tb = new.astype(jnp.bfloat16)
        th[rows, pl.ds(0, nf)] = tb
        th_copy(p).start()
        xb = (new - mu_ref[...]).astype(jnp.bfloat16)
        pm = lax.dot_general(ut_ref[...], xb, (((1,), (1,)), ((), ())), preferred_element_type=jnp.float32)
        half = lax.div(p, 3)
        for h in range(2):
            q = lax.rem(p, 3) * 2 + h
            pmb[half, pl.ds(pl.multiple_of(q * 16, 16), 16), :] = pm[:, h * B:(h + 1) * B]
            t = tb[h * B:(h + 1) * B, :].astype(jnp.float32)
            sq = t * t
            tot = sq[:, 0:B]
            for m in range(1, nf // B):
                tot = tot + sq[:, m * B:(m + 1) * B]
            dsrc[pl.ds(p * 2 + h, 1), :] = jnp.sum(tot.T, axis=0, keepdims=True)

    barrier = pltpu.get_barrier_semaphore()
    for o in range(1, 16):
        e = lax.rem(me + o, 16)
        pl.semaphore_signal(barrier, inc=1, device_id=(ens, lax.div(e, 4), lax.rem(e, 4)), device_id_type=MESH)
    for p in range(UP):
        load_copy(p).start()
    pmb[...] = jnp.zeros_like(pmb)
    dsrc[...] = jnp.zeros_like(dsrc)
    pl.semaphore_wait(barrier, 15)

    @pl.loop(0, UP)
    def _(p):
        load_copy(p).wait()
        rows = pl.ds(pl.multiple_of(p * ROW, ROW), ROW)
        post(p, theta[rows, :])

    @pl.loop(0, NUM_STEPS)
    def _(step):
        for e in range(8):
            mine = me == (e // 4) * 12 + e % 4

            @pl.when(mine)
            def _():
                dg_local().start()

            @pl.when(jnp.logical_not(mine))
            def _():
                dg_copy(e).start()

        pm_copy().start()
        sacc[...] = jnp.zeros_like(sacc)

        @pl.loop(0, UP)
        def _(p):
            th_copy(p).wait()

        pm_copy().wait()

        @pl.loop(0, 5)
        def _(k):
            for d in range(2):
                gy[d, k] = gram(slot_yf(k, d, 1 - y, c))
            for d in range(2):
                y_copy(d, k).start()

        @pl.loop(0, ITERS)
        def _(g):
            for d in range(2):
                pos = z if d else 3 - z
                i = g - LAG * pos

                @pl.when((i >= 0) & (i < CH))
                def _():
                    n = slot_chain(i, d, y, c)

                    @pl.when(n < NB)
                    def _():
                        gsrc[d, i] = gram(n)

                    if d == 0:
                        @pl.when(n >= NB)
                        def _():
                            gsrc[d, i] = pmb[c] + pmrecv[...]

                    @pl.when(i >= 10)
                    def _():
                        y_copy(d, i - 10).wait_recv()
                        gsrc[d, i] = gsrc[d, i] + yrecv[d, i - 10]

                    @pl.when(pos > 0)
                    def _():
                        z_copy(d, i).wait_recv()
                        gsrc[d, i] = gsrc[d, i] + zrecv[d, i]

            for d in range(2):
                pos = z if d else 3 - z
                i = g - LAG * pos

                @pl.when((i >= 0) & (i < CH))
                def _():
                    @pl.when(pos < 3)
                    def _():
                        z_copy(d, i).start()

                    @pl.when((pos == 3) & (i < 10) & (lax.rem(i, 2) != y))
                    def _():
                        ye_copy(lax.div(i, 2), i).start()

            i = g - FIN0

            @pl.when(corner & (i >= 0) & (i < CH))
            def _():
                @pl.when(i == 0)
                def _():
                    tot = jnp.zeros((16, B), jnp.float32)
                    for e in range(16):
                        pltpu.make_async_copy(dsrc, dgather.at[e], dg_r.at[e]).wait()
                        tot = tot + dgather[e]
                    dsum[...] = tot

                @pl.when((i >= 10) | (lax.rem(i, 2) == y))
                def _():
                    @pl.when(i < 10)
                    def _():
                        k = lax.div(i, 2)
                        ye_copy(k, i).wait_recv()
                        gsrc[dc, i] = gsrc[dc, i] + yend[k]

                    n = slot_chain(i, dc, y, c)
                    bi, bj = _block(n)
                    dst_r = pl.ds(pl.multiple_of(bi * B, B), B)
                    dst_c = pl.ds(pl.multiple_of(bj * B, B), B)

                    @pl.when(n < NB)
                    def _():
                        gi = jnp.broadcast_to(dsum[pl.ds(bi, 1), :], (B, B)).T
                        gj = dsum[pl.ds(bj, 1), :]
                        sq = jnp.maximum(gi + gj - 2.0 * gsrc[dc, i], 0.0)
                        kk = jnp.exp(sq * (-1.0 / bandwidth))
                        kf[dst_r, dst_c] = kk.astype(jnp.bfloat16)
                        sacc[pl.ds(bj, 1), :] = sacc[pl.ds(bj, 1), :] + jnp.sum(kk, axis=0, keepdims=True)

                        @pl.when(n >= NP)
                        def _():
                            sacc[pl.ds(bi, 1), :] = sacc[pl.ds(bi, 1), :] + jnp.sum(kk.T, axis=0, keepdims=True)

                    @pl.when(n >= NB)
                    def _():
                        kf[dst_r, dst_c] = gsrc[dc, i].astype(jnp.bfloat16)

                    @pl.when(i < 10)
                    def _():
                        kyz_copy(lax.div(i, 2), y).start()

                    @pl.when(i >= 10)
                    def _():
                        ky_copy(dc, i - 10, y).start()

                @pl.when(i == CH - 1)
                def _():
                    for e in range(16):
                        @pl.when(me == e)
                        def _():
                            sg_local().start()

                        @pl.when(me != e)
                        def _():
                            sg_copy(e).start()

            for d in range(2):
                dist = 3 - z if d else z
                i = g - AG0 - LAG2 * dist

                @pl.when((i >= 0) & (i < CH))
                def _():
                    @pl.when((dist == 0) & (i < 10) & (lax.rem(i, 2) != y))
                    def _():
                        kyz_copy(lax.div(i, 2), 1 - y).wait_recv()

                    @pl.when(dist > 0)
                    def _():
                        kz_copy(d, i).wait_recv()

                    @pl.when(dist < 3)
                    def _():
                        kz_copy(d, i).start()

                    @pl.when((dist > 0) & (i >= 10))
                    def _():
                        ky_copy(d, i - 10, y).start()

                    kd_copy(d, i, c).start()
                    flip(slot_chain(i, d, y, c))

                k = i - OUT2 - 10

                @pl.when((k >= 0) & (k < 5))
                def _():
                    ky_copy(d, k, 1 - y).wait_recv()
                    ke_copy(d, k, c).start()
                    flip(slot_yf(k, d, 1 - y, c))

                j = i - DIE

                @pl.when((j >= 0) & (j < CH))
                def _():
                    kd_copy(d, j, 1 - c).wait_recv()
                    flip(slot_chain(j, d, y, 1 - c))

                m = k - DIE

                @pl.when((m >= 0) & (m < 5))
                def _():
                    ke_copy(d, m, 1 - c).wait_recv()
                    flip(slot_yf(m, d, 1 - y, 1 - c))

            p = g - (AG0 + 3 * LAG2 + DIE + 2)

            @pl.when((p >= 0) & (p < UP))
            def _():
                rows = pl.ds(pl.multiple_of(p * ROW, ROW), ROW)
                q = lax.rem(p, 3)
                half = lax.div(p, 3)
                hcol = pl.ds(pl.multiple_of(half * B, B), B)
                pmt = jnp.concatenate(
                    [kf[pl.ds(pl.multiple_of(NP * B + (q * 2 + h) * 16, 16), 16), hcol] for h in range(2)], axis=1
                )
                low = lax.dot_general(
                    pmt.astype(jnp.float32).T.astype(jnp.bfloat16),
                    ut_ref[...],
                    (((1,), (0,)), ((), ())),
                    preferred_element_type=jnp.float32,
                )
                cur = theta[rows, :]
                grad = -((cur - mu_ref[...]) * lam_ref[...] + low)
                a_ref[rows, :] = (grad - rep * cur).astype(jnp.bfloat16)

        for e in range(8):
            @pl.when(me != (e // 4) * 12 + e % 4)
            def _():
                dg_copy(e).wait_send()

        @pl.loop(0, 5)
        def _(k):
            for d in range(2):
                y_copy(d, k).wait_send()
                ke_copy(d, k, c).wait_send()
                ky_copy(d, k, y).wait_send()

            @pl.when(corner)
            def _():
                ye_copy(k, 2 * k + 1 - y).wait_send()
                kyz_copy(k, y).wait_send()

        @pl.loop(0, CH)
        def _(i):
            for d in range(2):
                pos = z if d else 3 - z

                @pl.when(pos < 3)
                def _():
                    z_copy(d, i).wait_send()

                @pl.when(pos > 0)
                def _():
                    kz_copy(d, i).wait_send()

                kd_copy(d, i, c).wait_send()

        @pl.when(corner)
        def _():
            for e in range(16):
                @pl.when(me != e)
                def _():
                    sg_copy(e).wait_send()

        tot = jnp.zeros((16, B), jnp.float32)
        for e in range(8):
            pltpu.make_async_copy(sacc, sgather.at[e], sg_r.at[e]).wait()
            tot = tot + sgather[e]
        ssum[...] = tot

        @pl.loop(0, UP)
        def _(p):
            rows = pl.ds(pl.multiple_of(p * ROW, ROW), ROW)
            acc = jnp.dot(kf[rows, :], a_ref[...], preferred_element_type=jnp.float32)
            cur = theta[rows, :]
            col = jnp.concatenate(
                [jnp.broadcast_to(ssum[pl.ds(p * 2 + h, 1), :], (B, B)).T[:, 0:1] for h in range(2)], axis=0
            )
            phi = (acc + (rep * col) * cur) * (1.0 / n_part)
            new = cur + step_size * phi
            theta[rows, :] = new

            @pl.when(step < NUM_STEPS - 1)
            def _():
                post(p, new)

            @pl.when(step == NUM_STEPS - 1)
            def _():
                out_copy(p).start()

    @pl.loop(0, UP)
    def _(p):
        out_copy(p).wait()


def solution(mesh):
    def run_steps(particles, prec_diag, mean_vec, low_rank):
        width = particles.shape[1]

        def local_steps(current, prec_loc, mean_loc, fac_loc):
            n_part, nf = current.shape
            dma = pltpu.SemaphoreType.DMA
            f32, bf16 = jnp.float32, jnp.bfloat16
            vmem = pltpu.VMEM
            return pl.pallas_call(
                functools.partial(kernel, width),
                out_shape=jax.ShapeDtypeStruct((n_part, nf), f32),
                in_specs=[pl.BlockSpec(memory_space=pl.ANY)] + [pl.BlockSpec(memory_space=pltpu.VMEM)] * 3,
                out_specs=pl.BlockSpec(memory_space=pl.ANY),
                scratch_shapes=[
                    vmem((n_part, nf), f32),
                    vmem((n_part, 2 * nf), bf16),
                    vmem((n_part, nf), bf16),
                    vmem((n_part + B, n_part), bf16),
                    vmem((2, CH, B, B), f32),
                    vmem((2, 5, B, B), f32),
                    vmem((2, CH, B, B), f32),
                    vmem((2, 5, B, B), f32),
                    vmem((5, B, B), f32),
                    vmem((2, B, B), f32),
                    vmem((B, B), f32),
                    vmem((16, B), f32),
                    vmem((16, 16, B), f32),
                    vmem((16, B), f32),
                    vmem((16, B), f32),
                    vmem((8, 16, B), f32),
                    vmem((16, B), f32),
                    dma((UP,)), dma((UP,)), dma((UP,)), dma((UP,)), dma, dma, dma((8,)), dma((16,)), dma((16,)), dma((8,)),
                    dma((2, CH)), dma((2, CH)), dma((2, 5)), dma((2, 5)), dma((5,)), dma((5,)),
                    dma((2, CH)), dma((2, CH)), dma((5,)), dma((5,)), dma((2, 5)), dma((2, 5)),
                    dma((2, CH)), dma((2, CH)), dma((2, 5)), dma((2, 5)),
                ],
                compiler_params=pltpu.CompilerParams(
                    collective_id=0, has_side_effects=True, vmem_limit_bytes=56 * 1024 * 1024
                ),
                name="svgd",
            )(current, prec_loc.reshape(1, nf), mean_loc.reshape(1, nf), fac_loc.T)

        sharded = jax.shard_map(
            local_steps,
            mesh=mesh,
            in_specs=(P("ens", FEAT_AXES), P(LEAD_AXES), P(LEAD_AXES), P(LEAD_AXES, None)),
            out_specs=P("ens", FEAT_AXES),
            check_vma=False,
        )
        return sharded(particles, prec_diag, mean_vec, low_rank)

    return run_steps
```

time: 777 us -> 233 us (0.30)
  waiting for transfers between devices: 323 us -> 0 us
  blocking collectives: 247 us -> 0 us
  Pallas kernels: 0 us -> 225 us
  matrix products: 95.7 us -> 0 us
  local copies, waits for them, and re-layouts: 78.7 us -> 7.91 us
  other arithmetic: 16.2 us -> 0 us
  between operations: 13.2 us -> 0.01 us
    psum x3 -> x0, waiting for transfers between devices: 323 us -> none  [local_steps(): gram_full = lax.psum(gram_part, FEAT_AXES)]
    psum x3 -> x0, blocking collectives: 247 us -> none  [local_steps(): proj_full = lax.psum(proj_part, FEAT_AXES)]
    pallas_call x0 -> x1, Pallas kernels: none -> 225 us  [local_steps(): pl.pallas_call(functools.partial(kernel, width), out_shape=jax.ShapeDtype...]
    dot_general x9 -> x0, matrix products: 95.7 us -> none  [the longest x3 50.3 us: local_steps(): jnp.dot(kernel.astype(jnp.bfloat16), drive_term.astype(jnp.bfloat16), pre...]
    gather x3 -> x0, local copies, waits for them, and re-layouts: 78.1 us -> none  [local_steps(): gram_diag = jnp.diagonal(gram_full)]
    reduce_sum x3 -> x0, other arithmetic: 16.1 us -> none  [local_steps(): jnp.sum(kernel, axis=1)[:, None]]
  transfers between devices with their start and end apart: 3 -> 0, of which waited for: 3 -> 0; matrix products, arithmetic and copies ran while one was open for 1% -> 0% of each run, Pallas kernels for 0% -> 0%
where the time goes in v1:
time: 233 us
  Pallas kernels  225 us (97%)
  local copies, waits for them, and re-layouts  7.91 us (3%)
    pallas_call x1, Pallas kernels, local_steps(): pl.pallas_call(functools.partial(kernel, width), out_shape=jax.ShapeDtype...  225 us
    unnamed x1, local copies, waits for them, and re-layouts  5.36 us

profile of v1, /device:TPU:0, one launch (start us, length us, event | category | flops | bytes accessed | tf_op | source)
XLA Modules:
  0.0 232.6 jit_solution(297258555963537282)
XLA Ops:
  0.0 1.3 reshape.6.lam_ref
  1.3 1.3 reshape.7.mu_ref
  2.5 224.7 %svgd.1 = f32[1536,896]{1,0:T(8,128)} custom-call(f32[1536,896]{1,0:T(8,128)} %x_hbm.1, f32[1,896]{1,0:T(1,128)} %reshape.6.lam_ref, f32[1,896]{1,0:T(1,128)} %reshape.7.mu_ref, bf16[16,896]{1,0:T(8,128)(2,1)} %bitcast.1), custom_call_target="tpu_custom_call" | custom-call | tf_op jit(solution)/shard_map/svgd/pallas_call | solution.py:472
  227.2 5.4 %copy.6 = f32[1536,896]{1,0:T(8,128)} copy(f32[1536,896]{1,0:T(8,128)} %svgd.1) | data formatting | bytes 11010048

commit v2 on v1

--- a/solution.py
+++ b/solution.py
@@ -19,11 +19,11 @@
 NB = 78
 ROW = 256
 UP = 6
-LAG = 2
-END = 2
-OUT1 = 2
-LAG2 = 2
-OUT2 = 2
+LAG = 3
+END = 3
+OUT1 = 3
+LAG2 = 3
+OUT2 = 3
 DIE = 2
 FIN0 = 3 * LAG + END
 AG0 = FIN0 + OUT1

time: 233 us -> 217 us (0.931)
  Pallas kernels: 225 us -> 209 us
    pallas_call x1, Pallas kernels: 225 us -> 209 us  [local_steps(): pl.pallas_call(functools.partial(kernel, width), out_shape=jax.ShapeDtype...]
where the time goes in v2:
time: 217 us
  Pallas kernels  209 us (96%)
  local copies, waits for them, and re-layouts  7.91 us (4%)
    pallas_call x1, Pallas kernels, local_steps(): pl.pallas_call(functools.partial(kernel, width), out_shape=jax.ShapeDtype...  209 us
    unnamed x1, local copies, waits for them, and re-layouts  5.36 us

profile of v2, /device:TPU:0, one launch (start us, length us, event | category | flops | bytes accessed | tf_op | source)
XLA Modules:
  0.0 217.2 jit_solution(14675134921738841682)
XLA Ops:
  0.0 1.3 reshape.6.lam_ref
  1.3 1.3 reshape.7.mu_ref
  2.5 209.3 %svgd.1 = f32[1536,896]{1,0:T(8,128)} custom-call(f32[1536,896]{1,0:T(8,128)} %x_hbm.1, f32[1,896]{1,0:T(1,128)} %reshape.6.lam_ref, f32[1,896]{1,0:T(1,128)} %reshape.7.mu_ref, bf16[16,896]{1,0:T(8,128)(2,1)} %bitcast.1), custom_call_target="tpu_custom_call" | custom-call | tf_op jit(solution)/shard_map/svgd/pallas_call | solution.py:472
  211.9 5.4 %copy.6 = f32[1536,896]{1,0:T(8,128)} copy(f32[1536,896]{1,0:T(8,128)} %svgd.1) | data formatting | bytes 11010048

commit v3 on v2

--- a/solution.py
+++ b/solution.py
@@ -19,12 +19,12 @@
 NB = 78
 ROW = 256
 UP = 6
-LAG = 3
-END = 3
-OUT1 = 3
-LAG2 = 3
-OUT2 = 3
-DIE = 2
+LAG = 4
+END = 4
+OUT1 = 4
+LAG2 = 4
+OUT2 = 4
+DIE = 3
 FIN0 = 3 * LAG + END
 AG0 = FIN0 + OUT1
 CH = 15

time: 217 us -> 225 us (1.037)
  Pallas kernels: 209 us -> 217 us
    pallas_call x1, Pallas kernels: 209 us -> 217 us  [local_steps(): pl.pallas_call(functools.partial(kernel, width), out_shape=jax.ShapeDtype...]
where the time goes in v3:
time: 225 us
  Pallas kernels  217 us (96%)
  local copies, waits for them, and re-layouts  7.91 us (4%)
    pallas_call x1, Pallas kernels, local_steps(): pl.pallas_call(functools.partial(kernel, width), out_shape=jax.ShapeDtype...  217 us
    unnamed x1, local copies, waits for them, and re-layouts  5.36 us

profile of v3, /device:TPU:0, one launch (start us, length us, event | category | flops | bytes accessed | tf_op | source)
XLA Modules:
  0.0 225.2 jit_solution(7896558768110178199)
XLA Ops:
  0.0 1.3 reshape.6.lam_ref
  1.3 1.3 reshape.7.mu_ref
  2.5 217.3 %svgd.1 = f32[1536,896]{1,0:T(8,128)} custom-call(f32[1536,896]{1,0:T(8,128)} %x_hbm.1, f32[1,896]{1,0:T(1,128)} %reshape.6.lam_ref, f32[1,896]{1,0:T(1,128)} %reshape.7.mu_ref, bf16[16,896]{1,0:T(8,128)(2,1)} %bitcast.1), custom_call_target="tpu_custom_call" | custom-call | tf_op jit(solution)/shard_map/svgd/pallas_call | solution.py:472
  219.8 5.4 %copy.6 = f32[1536,896]{1,0:T(8,128)} copy(f32[1536,896]{1,0:T(8,128)} %svgd.1) | data formatting | bytes 11010048

commit v4 on v3

v4 whole, which is shorter than its diff:
```python
import functools

import jax
import jax.numpy as jnp
from jax import lax
from jax.experimental import pallas as pl
from jax.experimental.pallas import tpu as pltpu
from jax.sharding import PartitionSpec as P

NUM_STEPS = 3
BAND_SCALE = 4.0
STEP_SCALE = 0.4
FEAT_AXES = ("slab", "feat")
LEAD_AXES = ("ens", "slab", "feat")
MESH = pl.DeviceIdType.MESH

B = 128
ROW = 256
UP = 6
START = 2
LAG = 3
END = 2
OUT1 = 2
LAG2 = 4
OUT2 = 4
DIE = 3
YF0 = 3
FIN0 = START + 3 * LAG + END
AG0 = FIN0 + OUT1
CH = 15
PM = 6
DRV0 = AG0 + 3 * LAG2 + PM + 1 + DIE + 1
ITERS = AG0 + 3 * LAG2 + CH + OUT2 + DIE


def _ref(k, t, d, ey, c):
    f = lax.div(k, 4)
    return k * 16 + (1 - f) * (t * 8 + d * 4 + ey * 2 + c) + f * (t * 4 + d * 2 + ey)


def _block(n):
    p = lax.div(n + 126, B) + lax.div(n + 120, B) + lax.div(n + 110, B) + lax.div(n + 96, B) + lax.div(n + 78, B)
    r = n - 2 * p * p
    i = lax.div(r, 2)
    j = 2 * p + lax.rem(r, 2)
    return i, j, p, 1 - jnp.minimum(j - i, 1)


def _clip(i, n):
    return jnp.minimum(jnp.maximum(i, 0), n - 1)


def _span(i):
    return pl.ds(pl.multiple_of(i * B, B), B)


def _home(n):
    i, j, p, e = _block(n)
    return _span(i + e * (2 * UP - i)), _span(j + e * (p - j))


def kernel(width, x_hbm, lam_ref, mu_ref, ut_ref, o_hbm, theta, th, a_ref, kf, gsrc, gy, zrecv, yrecv, yend, pmb, pmrecv,
           ps, pzr, pye, pmf,
           dsrc, dgather, dsum, sacc, sgather, ssum, ld, od, thd_s, thd_r, pm_s, pm_r, dg_s, dg_r, sg_s, sg_r,
           zs, zr, ys, yr, ye_s, ye_r, kz_s, kz_r, kyz_s, kyz_r, ky_s, ky_r, kd_s, kd_r, ke_s, ke_r,
           pz_s, pz_r, pye_s, pye_r, pky_s, pky_r, pkz_s, pkz_r, pkd_s, pkd_r):
    nf = theta.shape[1]
    n_part = theta.shape[0]
    bandwidth = BAND_SCALE * width
    step_size = STEP_SCALE * width
    rep = 2.0 / bandwidth
    f32, bf16 = jnp.float32, jnp.bfloat16
    ens = lax.axis_index("ens")
    z = lax.axis_index("slab")
    feat = lax.axis_index("feat")
    y = lax.div(feat, 2)
    c = lax.rem(feat, 2)
    me = z * 4 + feat
    ypart = (ens, z, (1 - y) * 2 + c)
    dpart = (ens, z, y * 2 + 1 - c)
    dc = lax.div(z, 3)
    corner = lax.rem(z, 3) == 0
    own8 = (dc * 2 + y) * 2 + c
    rounds = 4 + c
    chain = 3 * rounds
    other_chain = 27 - chain

    def rcopy(src, dst, s, r, dev):
        return pltpu.make_async_remote_copy(src_ref=src, dst_ref=dst, send_sem=s, recv_sem=r, device_id=dev, device_id_type=MESH)

    def zdev(dz):
        return (ens, z + dz, feat)

    def place(i, cc):
        zf = 8 + 2 * cc
        w = lax.div(i, zf)
        return w, (1 - w) * lax.div(i, 2) + w * (i - zf), lax.rem(i, 2)

    def num_chain(i, d, cc):
        w, k, e = place(i, cc)
        return _ref(k, w, d, (1 - w) * e + w * y, cc)

    def panel(p):
        return pl.ds(pl.multiple_of(p * ROW, ROW), ROW)

    def load_copy(p):
        return pltpu.make_async_copy(x_hbm.at[panel(p)], theta.at[panel(p)], ld.at[p])

    def out_copy(p):
        return pltpu.make_async_copy(theta.at[panel(p)], o_hbm.at[panel(p)], od.at[p])

    def th_copy(p):
        return rcopy(th.at[panel(p), pl.ds(0, nf)], th.at[panel(p), pl.ds(nf, nf)], thd_s.at[p], thd_r.at[p], dpart)

    def pm_copy():
        return rcopy(pmb.at[1 - c], pmrecv, pm_s, pm_r, dpart)

    def dg_copy(e):
        return rcopy(dsrc, dgather.at[me], dg_s.at[e], dg_r.at[me], (ens, (e // 4) * 3, e % 4))

    def dg_local():
        return pltpu.make_async_copy(dsrc, dgather.at[me], dg_r.at[me])

    def sg_copy(e):
        return rcopy(sacc, sgather.at[own8], sg_s.at[e], sg_r.at[own8], (ens, e // 4, e % 4))

    def sg_local():
        return pltpu.make_async_copy(sacc, sgather.at[own8], sg_r.at[own8])

    def z_copy(d, i):
        return rcopy(gsrc.at[d, i], zrecv.at[d, i], zs.at[d, i], zr.at[d, i], zdev(2 * d - 1))

    def y_copy(d, k):
        return rcopy(gy.at[d, k], yrecv.at[d, k], ys.at[d, k], yr.at[d, k], ypart)

    def ye_copy(k, i):
        return rcopy(gsrc.at[dc, i], yend.at[k], ye_s.at[k], ye_r.at[k], ypart)

    def kf_copy(n, s, r, dev):
        rows, cols = _home(n)
        return rcopy(kf.at[rows, cols], kf.at[rows, cols], s, r, dev)

    def kz_copy(d, i):
        return kf_copy(num_chain(i, d, c), kz_s.at[d, i], kz_r.at[d, i], zdev(1 - 2 * d))

    def kyz_copy(k, ey):
        return kf_copy(_ref(k, 0, dc, ey, c), kyz_s.at[k], kyz_r.at[k], ypart)

    def ky_copy(d, k, yy):
        return kf_copy(_ref(k, 1, d, yy, c), ky_s.at[d, k], ky_r.at[d, k], ypart)

    def kd_copy(d, i, cc):
        return kf_copy(num_chain(i, d, cc), kd_s.at[d, i], kd_r.at[d, i], dpart)

    def ke_copy(d, k, cc):
        return kf_copy(_ref(k, 1, d, 1 - y, cc), ke_s.at[d, k], ke_r.at[d, k], dpart)

    def pz_copy(d, e):
        return rcopy(ps.at[d, e], pzr.at[d, e], pz_s.at[d, e], pz_r.at[d, e], zdev(2 * d - 1))

    def pye_copy(e):
        return rcopy(ps.at[dc, e], pye, pye_s, pye_r, ypart)

    def pf_copy(d, e, cc, s, r, dev):
        return rcopy(pmf.at[cc, 2 * d + e], pmf.at[cc, 2 * d + e], s, r, dev)

    def pky_copy(e):
        return pf_copy(dc, e, c, pky_s, pky_r, ypart)

    def pkz_copy(d, e):
        return pf_copy(d, e, c, pkz_s.at[d, e], pkz_r.at[d, e], zdev(1 - 2 * d))

    def pkd_copy(d, e, cc):
        return pf_copy(d, e, cc, pkd_s.at[d, e], pkd_r.at[d, e], dpart)

    def low_tri():
        return lax.broadcasted_iota(jnp.int32, (B, B), 0) - lax.broadcasted_iota(jnp.int32, (B, B), 1)

    def unpack(kk):
        kt = kk.T
        tri = low_tri()
        return jnp.where(tri >= 0, kk, kt), jnp.where(tri < 0, kk, jnp.where(tri == 0, 1.0, kt))

    def mirror(n):
        i, j, p, e = _block(n)

        @pl.when(e == 0)
        def _():
            kf[_span(j), _span(i)] = kf[_span(i), _span(j)].astype(f32).T.astype(bf16)

        @pl.when(e == 1)
        def _():
            first, second = unpack(kf[pl.ds(2 * UP * B, B), _span(p)].astype(f32))
            kf[_span(2 * p), _span(2 * p)] = first.astype(bf16)
            kf[_span(2 * p + 1), _span(2 * p + 1)] = second.astype(bf16)

    def dot_t(i, j):
        return lax.dot_general(th[_span(i), :], th[_span(j), :], (((1,), (1,)), ((), ())), preferred_element_type=f32)

    def gram(dst, n):
        i, j, p, e = _block(n)
        dst[...] = dot_t(i, j)

        @pl.when(e == 1)
        def _():
            dst[...] = jnp.where(low_tri() >= 0, dst[...], dot_t(2 * p + 1, 2 * p + 1))

    def post(p):
        new = theta[panel(p), :]
        tb = new.astype(bf16)
        th[panel(p), pl.ds(0, nf)] = tb
        xb = (new - mu_ref[...]).astype(bf16)
        pm = lax.dot_general(ut_ref[...], xb, (((1,), (1,)), ((), ())), preferred_element_type=f32)
        th_copy(p).start()
        half = lax.div(p, 3)
        for h in range(2):
            q = lax.rem(p, 3) * 2 + h
            pmb[half, pl.ds(pl.multiple_of(q * 16, 16), 16), :] = pm[:, h * B:(h + 1) * B]
            t = tb[h * B:(h + 1) * B, :].astype(f32)
            sq = t * t
            tot = sq[:, 0:B]
            for m in range(1, nf // B):
                tot = tot + sq[:, m * B:(m + 1) * B]
            dsrc[pl.ds(p * 2 + h, 1), :] = jnp.sum(tot.T, axis=0, keepdims=True)

    def row_sums():
        tot = jnp.zeros((16, B), f32)
        for e in range(8):
            pltpu.make_async_copy(sacc, sgather.at[e], sg_r.at[e]).wait()
            tot = tot + sgather[e]
        ssum[...] = tot

    def update(p):
        acc = jnp.dot(kf[panel(p), :], a_ref[...], preferred_element_type=f32)
        cur = theta[panel(p), :]
        col = jnp.concatenate(
            [jnp.broadcast_to(ssum[pl.ds(p * 2 + h, 1), :], (B, B)).T[:, 0:1] for h in range(2)], axis=0
        )
        phi = (acc + (rep * col) * cur) * (1.0 / n_part)
        theta[panel(p), :] = cur + step_size * phi

    barrier = pltpu.get_barrier_semaphore()
    for o in range(1, 16):
        e = lax.rem(me + o, 16)
        pl.semaphore_signal(barrier, inc=1, device_id=(ens, lax.div(e, 4), lax.rem(e, 4)), device_id_type=MESH)
    for p in range(UP):
        load_copy(p).start()
    pmb[...] = jnp.zeros_like(pmb)
    dsrc[...] = jnp.zeros_like(dsrc)
    pl.semaphore_wait(barrier, 15)

    @pl.loop(0, NUM_STEPS)
    def _(step):
        @pl.when(step > 0)
        def _():
            row_sums()

        sacc[...] = jnp.zeros_like(sacc)

        @pl.loop(0, ITERS)
        def _(g):
            gp = jnp.minimum(g, UP - 1)

            @pl.when(g < UP)
            def _():
                @pl.when(step == 0)
                def _():
                    load_copy(gp).wait()

                @pl.when(step > 0)
                def _():
                    update(gp)

                post(gp)

            @pl.when(g == UP - 1)
            def _():
                for e in range(8):
                    mine = me == (e // 4) * 12 + e % 4

                    @pl.when(mine)
                    def _():
                        dg_local().start()

                    @pl.when(jnp.logical_not(mine))
                    def _():
                        dg_copy(e).start()

                pm_copy().start()

            @pl.when((g >= 1) & (g <= UP))
            def _():
                th_copy(_clip(g - 1, UP)).wait()

            @pl.when(g == START + PM)
            def _():
                pm_copy().wait()

            v = g - YF0
            v_on = (v >= 0) & (v < 2 * rounds)
            v = _clip(v, 2 * rounds)

            @pl.when(v_on)
            def _():
                d, k = lax.rem(v, 2), lax.div(v, 2)
                gram(gy.at[d, k], _ref(k, 1, d, 1 - y, c))

            for d in range(2):
                pos = z if d else 3 - z
                i = g - START - LAG * pos
                on = (i >= 0) & (i < chain)
                i = _clip(i, chain)

                @pl.when(on)
                def _():
                    w, k, e = place(i, c)
                    gram(gsrc.at[d, i], _ref(k, w, d, (1 - w) * e + w * y, c))

                    @pl.when(w == 1)
                    def _():
                        y_copy(d, k).wait_recv()
                        gsrc[d, i] = gsrc[d, i] + yrecv[d, k]

                    @pl.when(pos > 0)
                    def _():
                        z_copy(d, i).wait_recv()
                        gsrc[d, i] = gsrc[d, i] + zrecv[d, i]

                    @pl.when((i >= PM) & (i < PM + 2))
                    def _():
                        rows = pl.ds(pl.multiple_of((2 * d + e) * 32, 32), 32)
                        ps[d, e] = pmb[c, rows, :] + pmrecv[rows, :]

                        @pl.when(pos > 0)
                        def _():
                            pz_copy(d, e).wait_recv()
                            ps[d, e] = ps[d, e] + pzr[d, e]

            @pl.when(v_on)
            def _():
                y_copy(lax.rem(v, 2), lax.div(v, 2)).start()

            for d in range(2):
                pos = z if d else 3 - z
                i = g - START - LAG * pos
                on = (i >= 0) & (i < chain)
                i = _clip(i, chain)

                @pl.when(on)
                def _():
                    w, k, e = place(i, c)
                    cross = (pos == 3) & (w == 0) & (e != y)
                    rides = (i >= PM) & (i < PM + 2)

                    @pl.when((pos < 3) & rides)
                    def _():
                        pz_copy(d, e).start()

                    @pl.when(pos < 3)
                    def _():
                        z_copy(d, i).start()

                    @pl.when(cross & rides)
                    def _():
                        pye_copy(e).start()

                    @pl.when(cross)
                    def _():
                        ye_copy(k, i).start()

            i = g - FIN0
            on = corner & (i >= 0) & (i < chain)
            i = _clip(i, chain)

            @pl.when(on)
            def _():
                @pl.when(i == 0)
                def _():
                    tot = jnp.zeros((16, B), f32)
                    for e in range(16):
                        pltpu.make_async_copy(dsrc, dgather.at[e], dg_r.at[e]).wait()
                        tot = tot + dgather[e]
                    dsum[...] = tot

                w, k, e = place(i, c)

                @pl.when((w == 1) | (e == y))
                def _():
                    @pl.when(w == 0)
                    def _():
                        ye_copy(k, i).wait_recv()
                        gsrc[dc, i] = gsrc[dc, i] + yend[k]

                    n = num_chain(i, dc, c)
                    bi, bj, bp, be = _block(n)

                    def kern(gi, gj):
                        sq = jnp.maximum(gi + gj - 2.0 * gsrc[dc, i], 0.0)
                        return jnp.exp(sq * (-1.0 / bandwidth))

                    def add_sums(q, blk):
                        sacc[pl.ds(q, 1), :] = sacc[pl.ds(q, 1), :] + jnp.sum(blk, axis=0, keepdims=True)

                    @pl.when(be == 0)
                    def _():
                        kk = kern(jnp.broadcast_to(dsum[pl.ds(bi, 1), :], (B, B)).T, dsum[pl.ds(bj, 1), :])
                        kf[_span(bi), _span(bj)] = kk.astype(bf16)
                        add_sums(bj, kk)
                        add_sums(bi, kk.T)

                    @pl.when(be == 1)
                    def _():
                        tri = low_tri() >= 0
                        ga = jnp.broadcast_to(dsum[pl.ds(2 * bp, 1), :], (B, B))
                        gb = jnp.broadcast_to(dsum[pl.ds(2 * bp + 1, 1), :], (B, B))
                        kk = kern(jnp.where(tri, ga.T, gb.T), jnp.where(tri, ga, gb))
                        kk = jnp.where(low_tri() == 0, 1.0, kk)
                        kf[pl.ds(2 * UP * B, B), _span(bp)] = kk.astype(bf16)
                        first, second = unpack(kk)
                        add_sums(2 * bp, first)
                        add_sums(2 * bp + 1, second)

                    @pl.when((i >= PM) & (i < PM + 2))
                    def _():
                        pye_copy(e).wait_recv()
                        pmf[c, 2 * dc + e] = (ps[dc, e] + pye[...]).astype(bf16)
                        pky_copy(e).start()

                    @pl.when(w == 0)
                    def _():
                        kyz_copy(k, y).start()

                    @pl.when(w == 1)
                    def _():
                        ky_copy(dc, k, y).start()

                @pl.when(i == chain - 1)
                def _():
                    for o in range(16):
                        @pl.when(me == o)
                        def _():
                            sg_local().start()

                        @pl.when(me != o)
                        def _():
                            sg_copy(o).start()

            for d in range(2):
                dist = 3 - z if d else z
                h = g - AG0 - LAG2 * dist
                on = (h >= 0) & (h < chain)
                i = _clip(h, chain)

                @pl.when(on)
                def _():
                    w, k, e = place(i, c)
                    turn = (dist == 0) & (w == 0) & (e != y)

                    @pl.when((i >= PM) & (i < PM + 2))
                    def _():
                        @pl.when(turn)
                        def _():
                            pky_copy(1 - y).wait_recv()

                        @pl.when(dist > 0)
                        def _():
                            pkz_copy(d, e).wait_recv()

                        @pl.when(dist < 3)
                        def _():
                            pkz_copy(d, e).start()

                        pkd_copy(d, e, c).start()

                    @pl.when(turn)
                    def _():
                        kyz_copy(k, 1 - y).wait_recv()

                    @pl.when(dist > 0)
                    def _():
                        kz_copy(d, i).wait_recv()

                    @pl.when(dist < 3)
                    def _():
                        kz_copy(d, i).start()

                    @pl.when((dist > 0) & (w == 1))
                    def _():
                        ky_copy(d, k, y).start()

                    kd_copy(d, i, c).start()
                    mirror(num_chain(i, d, c))

                k = h - OUT2 - 2 * rounds
                on = (k >= 0) & (k < rounds)
                k = _clip(k, rounds)

                @pl.when(on)
                def _():
                    ky_copy(d, k, 1 - y).wait_recv()
                    ke_copy(d, k, c).start()
                    mirror(_ref(k, 1, d, 1 - y, c))

                j = h - DIE
                on = (j >= 0) & (j < other_chain)
                j = _clip(j, other_chain)

                @pl.when(on)
                def _():
                    @pl.when((j >= PM) & (j < PM + 2))
                    def _():
                        pkd_copy(d, lax.rem(j, 2), 1 - c).wait_recv()

                    kd_copy(d, j, 1 - c).wait_recv()
                    mirror(num_chain(j, d, 1 - c))

                m = h - OUT2 - DIE - 2 * (9 - rounds)
                on = (m >= 0) & (m < 9 - rounds)
                m = _clip(m, 9 - rounds)

                @pl.when(on)
                def _():
                    ke_copy(d, m, 1 - c).wait_recv()
                    mirror(_ref(m, 1, d, 1 - y, 1 - c))

            p = g - DRV0
            on = (p >= 0) & (p < UP)
            p = _clip(p, UP)

            @pl.when(on)
            def _():
                q = lax.rem(p, 3) * 2
                half = lax.div(p, 3)
                pmt = jnp.concatenate(
                    [pmf[half, lax.div(q, 2), pl.ds(16 * h, 16), :] for h in range(2)], axis=1
                )
                low = lax.dot_general(
                    pmt.astype(f32).T.astype(bf16), ut_ref[...], (((1,), (0,)), ((), ())), preferred_element_type=f32
                )
                cur = theta[panel(p), :]
                grad = -((cur - mu_ref[...]) * lam_ref[...] + low)
                a_ref[panel(p), :] = (grad - rep * cur).astype(bf16)

        for e in range(8):
            @pl.when(me != (e // 4) * 12 + e % 4)
            def _():
                dg_copy(e).wait_send()

        for d in range(2):
            pos = z if d else 3 - z
            for e in range(2):
                @pl.when(pos < 3)
                def _():
                    pz_copy(d, e).wait_send()

                @pl.when(pos > 0)
                def _():
                    pkz_copy(d, e).wait_send()

                pkd_copy(d, e, c).wait_send()

        @pl.when(corner)
        def _():
            pye_copy(1 - y).wait_send()
            pky_copy(y).wait_send()

        @pl.loop(0, rounds)
        def _(k):
            for d in range(2):
                y_copy(d, k).wait_send()
                ke_copy(d, k, c).wait_send()
                ky_copy(d, k, y).wait_send()

            @pl.when(corner)
            def _():
                ye_copy(k, 2 * k + 1 - y).wait_send()
                kyz_copy(k, y).wait_send()

        @pl.loop(0, chain)
        def _(i):
            for d in range(2):
                pos = z if d else 3 - z

                @pl.when(pos < 3)
                def _():
                    z_copy(d, i).wait_send()

                @pl.when(pos > 0)
                def _():
                    kz_copy(d, i).wait_send()

                kd_copy(d, i, c).wait_send()

        @pl.when(corner)
        def _():
            for e in range(16):
                @pl.when(me != e)
                def _():
                    sg_copy(e).wait_send()

    row_sums()

    @pl.loop(0, UP)
    def _(p):
        update(p)
        out_copy(p).start()

    @pl.loop(0, UP)
    def _(p):
        out_copy(p).wait()


def solution(mesh):
    def run_steps(particles, prec_diag, mean_vec, low_rank):
        width = particles.shape[1]

        def local_steps(current, prec_loc, mean_loc, fac_loc):
            n_part, nf = current.shape
            dma = pltpu.SemaphoreType.DMA
            f32, bf16 = jnp.float32, jnp.bfloat16
            vmem = pltpu.VMEM
            return pl.pallas_call(
                functools.partial(kernel, width),
                out_shape=jax.ShapeDtypeStruct((n_part, nf), f32),
                in_specs=[pl.BlockSpec(memory_space=pl.ANY)] + [pl.BlockSpec(memory_space=pltpu.VMEM)] * 3,
                out_specs=pl.BlockSpec(memory_space=pl.ANY),
                scratch_shapes=[
                    vmem((n_part, nf), f32),
                    vmem((n_part, 2 * nf), bf16),
                    vmem((n_part, nf), bf16),
                    vmem((n_part + B, n_part), bf16),
                    vmem((2, CH, B, B), f32),
                    vmem((2, 5, B, B), f32),
                    vmem((2, CH, B, B), f32),
                    vmem((2, 5, B, B), f32),
                    vmem((5, B, B), f32),
                    vmem((2, B, B), f32),
                    vmem((B, B), f32),
                    vmem((2, 2, 32, B), f32),
                    vmem((2, 2, 32, B), f32),
                    vmem((32, B), f32),
                    vmem((2, 4, 32, B), bf16),
                    vmem((16, B), f32),
                    vmem((16, 16, B), f32),
                    vmem((16, B), f32),
                    vmem((16, B), f32),
                    vmem((8, 16, B), f32),
                    vmem((16, B), f32),
                    dma((UP,)), dma((UP,)), dma((UP,)), dma((UP,)), dma, dma, dma((8,)), dma((16,)), dma((16,)), dma((8,)),
                    dma((2, CH)), dma((2, CH)), dma((2, 5)), dma((2, 5)), dma((5,)), dma((5,)),
                    dma((2, CH)), dma((2, CH)), dma((5,)), dma((5,)), dma((2, 5)), dma((2, 5)),
                    dma((2, CH)), dma((2, CH)), dma((2, 5)), dma((2, 5)),
                    dma((2, 2)), dma((2, 2)), dma, dma, dma, dma, dma((2, 2)), dma((2, 2)), dma((2, 2)), dma((2, 2)),
                ],
                compiler_params=pltpu.CompilerParams(
                    collective_id=0, has_side_effects=True, vmem_limit_bytes=56 * 1024 * 1024
                ),
                name="svgd",
            )(current, prec_loc.reshape(1, nf), mean_loc.reshape(1, nf), fac_loc.T)

        sharded = jax.shard_map(
            local_steps,
            mesh=mesh,
            in_specs=(P("ens", FEAT_AXES), P(LEAD_AXES), P(LEAD_AXES), P(LEAD_AXES, None)),
            out_specs=P("ens", FEAT_AXES),
            check_vma=False,
        )
        return sharded(particles, prec_diag, mean_vec, low_rank)

    return run_steps
```

time: 225 us -> 201 us (0.89)
  Pallas kernels: 217 us -> 192 us
    pallas_call x1, Pallas kernels: 217 us -> 192 us  [local_steps(): pl.pallas_call(functools.partial(kernel, width), out_shape=jax.ShapeDtype...]
where the time goes in v4:
time: 201 us; the launch traced here: 200 us
  Pallas kernels  192 us (96%)
  local copies, waits for them, and re-layouts  7.91 us (4%)
    pallas_call x1, Pallas kernels, local_steps(): pl.pallas_call(functools.partial(kernel, width), out_shape=jax.ShapeDtype...  192 us
    unnamed x1, local copies, waits for them, and re-layouts  5.36 us

profile of v4, /device:TPU:0, one launch (start us, length us, event | category | flops | bytes accessed | tf_op | source)
XLA Modules:
  0.0 200.4 jit_solution(15010027559557343726)
XLA Ops:
  0.0 1.3 reshape.6.lam_ref
  1.3 1.3 reshape.7.mu_ref
  2.5 192.5 %svgd.1 = f32[1536,896]{1,0:T(8,128)} custom-call(f32[1536,896]{1,0:T(8,128)} %x_hbm.1, f32[1,896]{1,0:T(1,128)} %reshape.6.lam_ref, f32[1,896]{1,0:T(1,128)} %reshape.7.mu_ref, bf16[16,896]{1,0:T(8,128)(2,1)} %bitcast.1), custom_call_target="tpu_custom_call" | custom-call | tf_op jit(solution)/shard_map/svgd/pallas_call | solution.py:622
  195.0 5.4 %copy.6 = f32[1536,896]{1,0:T(8,128)} copy(f32[1536,896]{1,0:T(8,128)} %svgd.1) | data formatting | bytes 11010048

commit v5 on v4

--- a/solution.py
+++ b/solution.py
@@ -19,10 +19,10 @@
 UP = 6
 START = 2
 LAG = 3
-END = 2
-OUT1 = 2
-LAG2 = 4
-OUT2 = 4
+END = 3
+OUT1 = 3
+LAG2 = 5
+OUT2 = 5
 DIE = 3
 YF0 = 3
 FIN0 = START + 3 * LAG + END

time: 201 us -> 204 us (1.015)
  Pallas kernels: 192 us -> 196 us
    pallas_call x1, Pallas kernels: 192 us -> 196 us  [local_steps(): pl.pallas_call(functools.partial(kernel, width), out_shape=jax.ShapeDtype...]
where the time goes in v5:
time: 204 us
  Pallas kernels  196 us (96%)
  local copies, waits for them, and re-layouts  7.91 us (4%)
    pallas_call x1, Pallas kernels, local_steps(): pl.pallas_call(functools.partial(kernel, width), out_shape=jax.ShapeDtype...  196 us
    unnamed x1, local copies, waits for them, and re-layouts  5.36 us

profile of v5, /device:TPU:0, one launch (start us, length us, event | category | flops | bytes accessed | tf_op | source)
XLA Modules:
  0.0 204.2 jit_solution(4829074206492136006)
XLA Ops:
  0.0 1.3 reshape.6.lam_ref
  1.3 1.3 reshape.7.mu_ref
  2.5 196.2 %svgd.1 = f32[1536,896]{1,0:T(8,128)} custom-call(f32[1536,896]{1,0:T(8,128)} %x_hbm.1, f32[1,896]{1,0:T(1,128)} %reshape.6.lam_ref, f32[1,896]{1,0:T(1,128)} %reshape.7.mu_ref, bf16[16,896]{1,0:T(8,128)(2,1)} %bitcast.1), custom_call_target="tpu_custom_call" | custom-call | tf_op jit(solution)/shard_map/svgd/pallas_call | solution.py:622
  198.8 5.4 %copy.6 = f32[1536,896]{1,0:T(8,128)} copy(f32[1536,896]{1,0:T(8,128)} %svgd.1) | data formatting | bytes 11010048

commit v6 on v5

--- a/solution.py
+++ b/solution.py
@@ -81,7 +81,7 @@
     dc = lax.div(z, 3)
     corner = lax.rem(z, 3) == 0
     own8 = (dc * 2 + y) * 2 + c
-    rounds = 4 + c
+    rounds = 5 - c
     chain = 3 * rounds
     other_chain = 27 - chain
 
@@ -92,7 +92,7 @@
         return (ens, z + dz, feat)
 
     def place(i, cc):
-        zf = 8 + 2 * cc
+        zf = 10 - 2 * cc
         w = lax.div(i, zf)
         return w, (1 - w) * lax.div(i, 2) + w * (i - zf), lax.rem(i, 2)
 

time: 204 us -> 205 us (level)
  no operation moved by 1% of the time
where the time goes in v6:
time: 205 us
  Pallas kernels  197 us (96%)
  local copies, waits for them, and re-layouts  7.91 us (4%)
    pallas_call x1, Pallas kernels, local_steps(): pl.pallas_call(functools.partial(kernel, width), out_shape=jax.ShapeDtype...  197 us
    unnamed x1, local copies, waits for them, and re-layouts  5.36 us

profile of v6, /device:TPU:0, one launch (start us, length us, event | category | flops | bytes accessed | tf_op | source)
XLA Modules:
  0.0 204.6 jit_solution(6352741795974838460)
XLA Ops:
  0.0 1.3 reshape.6.lam_ref
  1.3 1.3 reshape.7.mu_ref
  2.5 196.7 %svgd.1 = f32[1536,896]{1,0:T(8,128)} custom-call(f32[1536,896]{1,0:T(8,128)} %x_hbm.1, f32[1,896]{1,0:T(1,128)} %reshape.6.lam_ref, f32[1,896]{1,0:T(1,128)} %reshape.7.mu_ref, bf16[16,896]{1,0:T(8,128)(2,1)} %bitcast.1), custom_call_target="tpu_custom_call" | custom-call | tf_op jit(solution)/shard_map/svgd/pallas_call | solution.py:622
  199.2 5.4 %copy.6 = f32[1536,896]{1,0:T(8,128)} copy(f32[1536,896]{1,0:T(8,128)} %svgd.1) | data formatting | bytes 11010048

commit v7 on v4

--- a/solution.py
+++ b/solution.py
@@ -54,12 +54,7 @@
     return pl.ds(pl.multiple_of(i * B, B), B)
 
 
-def _home(n):
-    i, j, p, e = _block(n)
-    return _span(i + e * (2 * UP - i)), _span(j + e * (p - j))
-
-
-def kernel(width, x_hbm, lam_ref, mu_ref, ut_ref, o_hbm, theta, th, a_ref, kf, gsrc, gy, zrecv, yrecv, yend, pmb, pmrecv,
+def kernel(width, x_hbm, lam_ref, mu_ref, ut_ref, o_hbm, theta, th, a_ref, kf, kc, ko, gsrc, gy, zrecv, yrecv, yend, pmb, pmrecv,
            ps, pzr, pye, pmf,
            dsrc, dgather, dsum, sacc, sgather, ssum, ld, od, thd_s, thd_r, pm_s, pm_r, dg_s, dg_r, sg_s, sg_r,
            zs, zr, ys, yr, ye_s, ye_r, kz_s, kz_r, kyz_s, kyz_r, ky_s, ky_r, kd_s, kd_r, ke_s, ke_r,
@@ -93,8 +88,9 @@
 
     def place(i, cc):
         zf = 8 + 2 * cc
-        w = lax.div(i, zf)
-        return w, (1 - w) * lax.div(i, 2) + w * (i - zf), lax.rem(i, 2)
+        w = _clip(i - zf + 1, 2)
+        h = lax.div(i, 2)
+        return w, h + w * (i - zf - h), i - 2 * h
 
     def num_chain(i, d, cc):
         w, k, e = place(i, cc)
@@ -136,24 +132,26 @@
     def ye_copy(k, i):
         return rcopy(gsrc.at[dc, i], yend.at[k], ye_s.at[k], ye_r.at[k], ypart)
 
-    def kf_copy(n, s, r, dev):
-        rows, cols = _home(n)
-        return rcopy(kf.at[rows, cols], kf.at[rows, cols], s, r, dev)
+    def kc_copy(d, i, cc, s, r, dev):
+        return rcopy(kc.at[cc, d, i], kc.at[cc, d, i], s, r, dev)
+
+    def ko_copy(d, k, cc, s, r, dev):
+        return rcopy(ko.at[cc, d, k], ko.at[cc, d, k], s, r, dev)
 
     def kz_copy(d, i):
-        return kf_copy(num_chain(i, d, c), kz_s.at[d, i], kz_r.at[d, i], zdev(1 - 2 * d))
-
-    def kyz_copy(k, ey):
-        return kf_copy(_ref(k, 0, dc, ey, c), kyz_s.at[k], kyz_r.at[k], ypart)
-
-    def ky_copy(d, k, yy):
-        return kf_copy(_ref(k, 1, d, yy, c), ky_s.at[d, k], ky_r.at[d, k], ypart)
+        return kc_copy(d, i, c, kz_s.at[d, i], kz_r.at[d, i], zdev(1 - 2 * d))
+
+    def kyz_copy(k, i):
+        return kc_copy(dc, i, c, kyz_s.at[k], kyz_r.at[k], ypart)
+
+    def ky_copy(d, k, i):
+        return rcopy(kc.at[c, d, i], ko.at[c, d, k], ky_s.at[d, k], ky_r.at[d, k], ypart)
 
     def kd_copy(d, i, cc):
-        return kf_copy(num_chain(i, d, cc), kd_s.at[d, i], kd_r.at[d, i], dpart)
+        return kc_copy(d, i, cc, kd_s.at[d, i], kd_r.at[d, i], dpart)
 
     def ke_copy(d, k, cc):
-        return kf_copy(_ref(k, 1, d, 1 - y, cc), ke_s.at[d, k], ke_r.at[d, k], dpart)
+        return ko_copy(d, k, cc, ke_s.at[d, k], ke_r.at[d, k], dpart)
 
     def pz_copy(d, e):
         return rcopy(ps.at[d, e], pzr.at[d, e], pz_s.at[d, e], pz_r.at[d, e], zdev(2 * d - 1))
@@ -181,16 +179,18 @@
         tri = low_tri()
         return jnp.where(tri >= 0, kk, kt), jnp.where(tri < 0, kk, jnp.where(tri == 0, 1.0, kt))
 
-    def mirror(n):
+    def settle(src, n):
         i, j, p, e = _block(n)
 
         @pl.when(e == 0)
         def _():
-            kf[_span(j), _span(i)] = kf[_span(i), _span(j)].astype(f32).T.astype(bf16)
+            blk = src[...]
+            kf[_span(i), _span(j)] = blk
+            kf[_span(j), _span(i)] = blk.astype(f32).T.astype(bf16)
 
         @pl.when(e == 1)
         def _():
-            first, second = unpack(kf[pl.ds(2 * UP * B, B), _span(p)].astype(f32))
+            first, second = unpack(src[...].astype(f32))
             kf[_span(2 * p), _span(2 * p)] = first.astype(bf16)
             kf[_span(2 * p + 1), _span(2 * p + 1)] = second.astype(bf16)
 
@@ -299,32 +299,65 @@
             v = g - YF0
             v_on = (v >= 0) & (v < 2 * rounds)
             v = _clip(v, 2 * rounds)
+            vk = lax.div(v, 2)
+            vd = v - 2 * vk
 
             @pl.when(v_on)
             def _():
-                d, k = lax.rem(v, 2), lax.div(v, 2)
-                gram(gy.at[d, k], _ref(k, 1, d, 1 - y, c))
-
+                gram(gy.at[vd, vk], _ref(vk, 1, vd, 1 - y, c))
+
+            state = []
             for d in range(2):
                 pos = z if d else 3 - z
                 i = g - START - LAG * pos
                 on = (i >= 0) & (i < chain)
                 i = _clip(i, chain)
+                w, k, e = place(i, c)
+                state.append((pos, on, i, w, k, e))
+
+            def send_sum(d):
+                pos, on, i, w, k, e = state[d]
 
                 @pl.when(on)
                 def _():
-                    w, k, e = place(i, c)
-                    gram(gsrc.at[d, i], _ref(k, w, d, (1 - w) * e + w * y, c))
-
+                    rides = (i >= PM) & (i < PM + 2)
+
+                    @pl.when(pos < 3)
+                    def _():
+                        @pl.when(rides)
+                        def _():
+                            pz_copy(d, e).start()
+
+                        z_copy(d, i).start()
+
+                    @pl.when((pos == 3) & (w == 0) & (e != y))
+                    def _():
+                        @pl.when(rides)
+                        def _():
+                            pye_copy(e).start()
+
+                        ye_copy(k, i).start()
+
+            for d in range(2):
+                pos, on, i, w, k, e = state[d]
+
+                @pl.when(on)
+                def _():
+                    gram(gsrc.at[d, i], _ref(k, w, d, e + w * (y - e), c))
+
+                if d == 0:
+                    @pl.when(v_on)
+                    def _():
+                        y_copy(vd, vk).start()
+                else:
+                    send_sum(0)
+
+                @pl.when(on)
+                def _():
                     @pl.when(w == 1)
                     def _():
                         y_copy(d, k).wait_recv()
                         gsrc[d, i] = gsrc[d, i] + yrecv[d, k]
-
-                    @pl.when(pos > 0)
-                    def _():
-                        z_copy(d, i).wait_recv()
-                        gsrc[d, i] = gsrc[d, i] + zrecv[d, i]
 
                     @pl.when((i >= PM) & (i < PM + 2))
                     def _():
@@ -336,120 +369,98 @@
                             pz_copy(d, e).wait_recv()
                             ps[d, e] = ps[d, e] + pzr[d, e]
 
-            @pl.when(v_on)
-            def _():
-                y_copy(lax.rem(v, 2), lax.div(v, 2)).start()
-
-            for d in range(2):
-                pos = z if d else 3 - z
-                i = g - START - LAG * pos
-                on = (i >= 0) & (i < chain)
-                i = _clip(i, chain)
-
-                @pl.when(on)
-                def _():
-                    w, k, e = place(i, c)
-                    cross = (pos == 3) & (w == 0) & (e != y)
-                    rides = (i >= PM) & (i < PM + 2)
-
-                    @pl.when((pos < 3) & rides)
-                    def _():
-                        pz_copy(d, e).start()
-
-                    @pl.when(pos < 3)
-                    def _():
-                        z_copy(d, i).start()
-
-                    @pl.when(cross & rides)
-                    def _():
-                        pye_copy(e).start()
-
-                    @pl.when(cross)
-                    def _():
-                        ye_copy(k, i).start()
+                    @pl.when(pos > 0)
+                    def _():
+                        z_copy(d, i).wait_recv()
+                        gsrc[d, i] = gsrc[d, i] + zrecv[d, i]
 
             i = g - FIN0
             on = corner & (i >= 0) & (i < chain)
             i = _clip(i, chain)
-
-            @pl.when(on)
-            def _():
-                @pl.when(i == 0)
-                def _():
-                    tot = jnp.zeros((16, B), f32)
-                    for e in range(16):
-                        pltpu.make_async_copy(dsrc, dgather.at[e], dg_r.at[e]).wait()
-                        tot = tot + dgather[e]
-                    dsum[...] = tot
-
-                w, k, e = place(i, c)
-
-                @pl.when((w == 1) | (e == y))
-                def _():
-                    @pl.when(w == 0)
-                    def _():
-                        ye_copy(k, i).wait_recv()
-                        gsrc[dc, i] = gsrc[dc, i] + yend[k]
-
-                    n = num_chain(i, dc, c)
-                    bi, bj, bp, be = _block(n)
-
-                    def kern(gi, gj):
-                        sq = jnp.maximum(gi + gj - 2.0 * gsrc[dc, i], 0.0)
-                        return jnp.exp(sq * (-1.0 / bandwidth))
-
-                    def add_sums(q, blk):
-                        sacc[pl.ds(q, 1), :] = sacc[pl.ds(q, 1), :] + jnp.sum(blk, axis=0, keepdims=True)
-
-                    @pl.when(be == 0)
-                    def _():
-                        kk = kern(jnp.broadcast_to(dsum[pl.ds(bi, 1), :], (B, B)).T, dsum[pl.ds(bj, 1), :])
-                        kf[_span(bi), _span(bj)] = kk.astype(bf16)
-                        add_sums(bj, kk)
-                        add_sums(bi, kk.T)
-
-                    @pl.when(be == 1)
-                    def _():
-                        tri = low_tri() >= 0
-                        ga = jnp.broadcast_to(dsum[pl.ds(2 * bp, 1), :], (B, B))
-                        gb = jnp.broadcast_to(dsum[pl.ds(2 * bp + 1, 1), :], (B, B))
-                        kk = kern(jnp.where(tri, ga.T, gb.T), jnp.where(tri, ga, gb))
-                        kk = jnp.where(low_tri() == 0, 1.0, kk)
-                        kf[pl.ds(2 * UP * B, B), _span(bp)] = kk.astype(bf16)
-                        first, second = unpack(kk)
-                        add_sums(2 * bp, first)
-                        add_sums(2 * bp + 1, second)
-
-                    @pl.when((i >= PM) & (i < PM + 2))
-                    def _():
-                        pye_copy(e).wait_recv()
-                        pmf[c, 2 * dc + e] = (ps[dc, e] + pye[...]).astype(bf16)
-                        pky_copy(e).start()
-
-                    @pl.when(w == 0)
-                    def _():
-                        kyz_copy(k, y).start()
-
-                    @pl.when(w == 1)
-                    def _():
-                        ky_copy(dc, k, y).start()
-
-                @pl.when(i == chain - 1)
-                def _():
-                    for o in range(16):
-                        @pl.when(me == o)
-                        def _():
-                            sg_local().start()
-
-                        @pl.when(me != o)
-                        def _():
-                            sg_copy(o).start()
-
+            w, k, e = place(i, c)
+
+            @pl.when(on & (i == 0))
+            def _():
+                tot = jnp.zeros((16, B), f32)
+                for o in range(16):
+                    pltpu.make_async_copy(dsrc, dgather.at[o], dg_r.at[o]).wait()
+                    tot = tot + dgather[o]
+                dsum[...] = tot
+
+            @pl.when(on & ((w == 1) | (e == y)))
+            def _():
+                @pl.when(w == 0)
+                def _():
+                    ye_copy(k, i).wait_recv()
+                    gsrc[dc, i] = gsrc[dc, i] + yend[k]
+
+                bi, bj, bp, be = _block(_ref(k, w, dc, y, c))
+
+                def kern(gi, gj):
+                    sq = jnp.maximum(gi + gj - 2.0 * gsrc[dc, i], 0.0)
+                    return jnp.exp(sq * (-1.0 / bandwidth))
+
+                def add_sums(q, blk):
+                    sacc[pl.ds(q, 1), :] = sacc[pl.ds(q, 1), :] + jnp.sum(blk, axis=0, keepdims=True)
+
+                @pl.when(be == 0)
+                def _():
+                    kk = kern(jnp.broadcast_to(dsum[pl.ds(bi, 1), :], (B, B)).T, dsum[pl.ds(bj, 1), :])
+                    kc[c, dc, i] = kk.astype(bf16)
+                    add_sums(bj, kk)
+                    add_sums(bi, kk.T)
+
+                @pl.when(be == 1)
+                def _():
+                    tri = low_tri() >= 0
+                    ga = jnp.broadcast_to(dsum[pl.ds(2 * bp, 1), :], (B, B))
+                    gb = jnp.broadcast_to(dsum[pl.ds(2 * bp + 1, 1), :], (B, B))
+                    kk = kern(jnp.where(tri, ga.T, gb.T), jnp.where(tri, ga, gb))
+                    kk = jnp.where(low_tri() == 0, 1.0, kk)
+                    kc[c, dc, i] = kk.astype(bf16)
+                    first, second = unpack(kk)
+                    add_sums(2 * bp, first)
+                    add_sums(2 * bp + 1, second)
+
+                @pl.when((i >= PM) & (i < PM + 2))
+                def _():
+                    pye_copy(e).wait_recv()
+                    pmf[c, 2 * dc + e] = (ps[dc, e] + pye[...]).astype(bf16)
+
+            send_sum(1)
+
+            @pl.when(on & ((w == 1) | (e == y)))
+            def _():
+                @pl.when((i >= PM) & (i < PM + 2))
+                def _():
+                    pky_copy(e).start()
+
+                @pl.when(w == 0)
+                def _():
+                    kyz_copy(k, i).start()
+
+                @pl.when(w == 1)
+                def _():
+                    ky_copy(dc, k, i).start()
+
+            @pl.when(on & (i == chain - 1))
+            def _():
+                for o in range(16):
+                    @pl.when(me == o)
+                    def _():
+                        sg_local().start()
+
+                    @pl.when(me != o)
+                    def _():
+                        sg_copy(o).start()
+
+            heard = []
             for d in range(2):
                 dist = 3 - z if d else z
                 h = g - AG0 - LAG2 * dist
                 on = (h >= 0) & (h < chain)
                 i = _clip(h, chain)
+                heard.append((h, on, i))
 
                 @pl.when(on)
                 def _():
@@ -474,54 +485,64 @@
 
                     @pl.when(turn)
                     def _():
-                        kyz_copy(k, 1 - y).wait_recv()
+                        kyz_copy(k, i).wait_recv()
 
                     @pl.when(dist > 0)
                     def _():
                         kz_copy(d, i).wait_recv()
 
+                        @pl.when(w == 1)
+                        def _():
+                            ky_copy(d, k, i).start()
+
                     @pl.when(dist < 3)
                     def _():
                         kz_copy(d, i).start()
 
-                    @pl.when((dist > 0) & (w == 1))
-                    def _():
-                        ky_copy(d, k, y).start()
-
                     kd_copy(d, i, c).start()
-                    mirror(num_chain(i, d, c))
 
                 k = h - OUT2 - 2 * rounds
-                on = (k >= 0) & (k < rounds)
-                k = _clip(k, rounds)
+
+                @pl.when((k >= 0) & (k < rounds))
+                def _():
+                    kk = _clip(k, rounds)
+                    ky_copy(d, kk, 0).wait_recv()
+                    ke_copy(d, kk, c).start()
+
+            for d in range(2):
+                h, on, i = heard[d]
 
                 @pl.when(on)
                 def _():
-                    ky_copy(d, k, 1 - y).wait_recv()
-                    ke_copy(d, k, c).start()
-                    mirror(_ref(k, 1, d, 1 - y, c))
+                    settle(kc.at[c, d, i], num_chain(i, d, c))
+
+                k = h - OUT2 - 2 * rounds
+
+                @pl.when((k >= 0) & (k < rounds))
+                def _():
+                    kk = _clip(k, rounds)
+                    settle(ko.at[c, d, kk], _ref(kk, 1, d, 1 - y, c))
 
                 j = h - DIE
-                on = (j >= 0) & (j < other_chain)
-                j = _clip(j, other_chain)
-
-                @pl.when(on)
-                def _():
-                    @pl.when((j >= PM) & (j < PM + 2))
-                    def _():
-                        pkd_copy(d, lax.rem(j, 2), 1 - c).wait_recv()
-
-                    kd_copy(d, j, 1 - c).wait_recv()
-                    mirror(num_chain(j, d, 1 - c))
+
+                @pl.when((j >= 0) & (j < other_chain))
+                def _():
+                    jj = _clip(j, other_chain)
+
+                    @pl.when((jj >= PM) & (jj < PM + 2))
+                    def _():
+                        pkd_copy(d, jj - 2 * lax.div(jj, 2), 1 - c).wait_recv()
+
+                    kd_copy(d, jj, 1 - c).wait_recv()
+                    settle(kc.at[1 - c, d, jj], num_chain(jj, d, 1 - c))
 
                 m = h - OUT2 - DIE - 2 * (9 - rounds)
-                on = (m >= 0) & (m < 9 - rounds)
-                m = _clip(m, 9 - rounds)
-
-                @pl.when(on)
-                def _():
-                    ke_copy(d, m, 1 - c).wait_recv()
-                    mirror(_ref(m, 1, d, 1 - y, 1 - c))
+
+                @pl.when((m >= 0) & (m < 9 - rounds))
+                def _():
+                    mm = _clip(m, 9 - rounds)
+                    ke_copy(d, mm, 1 - c).wait_recv()
+                    settle(ko.at[1 - c, d, mm], _ref(mm, 1, d, 1 - y, 1 - c))
 
             p = g - DRV0
             on = (p >= 0) & (p < UP)
@@ -569,12 +590,12 @@
             for d in range(2):
                 y_copy(d, k).wait_send()
                 ke_copy(d, k, c).wait_send()
-                ky_copy(d, k, y).wait_send()
+                ky_copy(d, k, 0).wait_send()
 
             @pl.when(corner)
             def _():
                 ye_copy(k, 2 * k + 1 - y).wait_send()
-                kyz_copy(k, y).wait_send()
+                kyz_copy(k, 0).wait_send()
 
         @pl.loop(0, chain)
         def _(i):
@@ -628,7 +649,9 @@
                     vmem((n_part, nf), f32),
                     vmem((n_part, 2 * nf), bf16),
                     vmem((n_part, nf), bf16),
-                    vmem((n_part + B, n_part), bf16),
+                    vmem((n_part, n_part), bf16),
+                    vmem((2, 2, CH, B, B), bf16),
+                    vmem((2, 2, 5, B, B), bf16),
                     vmem((2, CH, B, B), f32),
                     vmem((2, 5, B, B), f32),
                     vmem((2, CH, B, B), f32),

time: 201 us -> 201 us (level)
  no operation moved by 1% of the time
where the time goes in v7:
time: 201 us
  Pallas kernels  193 us (96%)
  local copies, waits for them, and re-layouts  7.91 us (4%)
    pallas_call x1, Pallas kernels, local_steps(): pl.pallas_call(functools.partial(kernel, width), out_shape=jax.ShapeDtype...  193 us
    unnamed x1, local copies, waits for them, and re-layouts  5.36 us

profile of v7, /device:TPU:0, one launch (start us, length us, event | category | flops | bytes accessed | tf_op | source)
XLA Modules:
  0.0 200.9 jit_solution(14825964572974667836)
XLA Ops:
  0.0 1.3 reshape.6.lam_ref
  1.3 1.3 reshape.7.mu_ref
  2.5 193.0 %svgd.1 = f32[1536,896]{1,0:T(8,128)} custom-call(f32[1536,896]{1,0:T(8,128)} %x_hbm.1, f32[1,896]{1,0:T(1,128)} %reshape.6.lam_ref, f32[1,896]{1,0:T(1,128)} %reshape.7.mu_ref, bf16[16,896]{1,0:T(8,128)(2,1)} %bitcast.1), custom_call_target="tpu_custom_call" | custom-call | tf_op jit(solution)/shard_map/svgd/pallas_call | solution.py:643
  195.5 5.4 %copy.6 = f32[1536,896]{1,0:T(8,128)} copy(f32[1536,896]{1,0:T(8,128)} %svgd.1) | data formatting | bytes 11010048

commit v8 on v7

--- a/solution.py
+++ b/solution.py
@@ -21,8 +21,8 @@
 LAG = 3
 END = 2
 OUT1 = 2
-LAG2 = 4
-OUT2 = 4
+LAG2 = 3
+OUT2 = 3
 DIE = 3
 YF0 = 3
 FIN0 = START + 3 * LAG + END
@@ -54,8 +54,8 @@
     return pl.ds(pl.multiple_of(i * B, B), B)
 
 
-def kernel(width, x_hbm, lam_ref, mu_ref, ut_ref, o_hbm, theta, th, a_ref, kf, kc, ko, gsrc, gy, zrecv, yrecv, yend, pmb, pmrecv,
-           ps, pzr, pye, pmf,
+def kernel(width, x_hbm, lam_in, mu_in, ut_ref, o_hbm, theta, th, a_ref, kf, kc, ko, gsrc, gy, zrecv, yrecv, yend, pmb, pmrecv,
+           ps, pzr, pye, pmf, lam_ref, mu_ref,
            dsrc, dgather, dsum, sacc, sgather, ssum, ld, od, thd_s, thd_r, pm_s, pm_r, dg_s, dg_r, sg_s, sg_r,
            zs, zr, ys, yr, ye_s, ye_r, kz_s, kz_r, kyz_s, kyz_r, ky_s, ky_r, kd_s, kd_r, ke_s, ke_r,
            pz_s, pz_r, pye_s, pye_r, pky_s, pky_r, pkz_s, pkz_r, pkd_s, pkd_r):
@@ -209,7 +209,7 @@
         new = theta[panel(p), :]
         tb = new.astype(bf16)
         th[panel(p), pl.ds(0, nf)] = tb
-        xb = (new - mu_ref[...]).astype(bf16)
+        xb = (new - mu_ref[0:1, 0:nf]).astype(bf16)
         pm = lax.dot_general(ut_ref[...], xb, (((1,), (1,)), ((), ())), preferred_element_type=f32)
         th_copy(p).start()
         half = lax.div(p, 3)
@@ -247,6 +247,9 @@
         load_copy(p).start()
     pmb[...] = jnp.zeros_like(pmb)
     dsrc[...] = jnp.zeros_like(dsrc)
+    for m in range(nf // B):
+        lam_ref[0:1, m * B:(m + 1) * B] = lam_in[m:m + 1, :]
+        mu_ref[0:1, m * B:(m + 1) * B] = mu_in[m:m + 1, :]
     pl.semaphore_wait(barrier, 15)
 
     @pl.loop(0, NUM_STEPS)
@@ -559,7 +562,7 @@
                     pmt.astype(f32).T.astype(bf16), ut_ref[...], (((1,), (0,)), ((), ())), preferred_element_type=f32
                 )
                 cur = theta[panel(p), :]
-                grad = -((cur - mu_ref[...]) * lam_ref[...] + low)
+                grad = -((cur - mu_ref[0:1, 0:nf]) * lam_ref[0:1, 0:nf] + low)
                 a_ref[panel(p), :] = (grad - rep * cur).astype(bf16)
 
         for e in range(8):
@@ -663,6 +666,8 @@
                     vmem((2, 2, 32, B), f32),
                     vmem((32, B), f32),
                     vmem((2, 4, 32, B), bf16),
+                    vmem((8, nf + B), f32),
+                    vmem((8, nf + B), f32),
                     vmem((16, B), f32),
                     vmem((16, 16, B), f32),
                     vmem((16, B), f32),
@@ -679,7 +684,7 @@
                     collective_id=0, has_side_effects=True, vmem_limit_bytes=56 * 1024 * 1024
                 ),
                 name="svgd",
-            )(current, prec_loc.reshape(1, nf), mean_loc.reshape(1, nf), fac_loc.T)
+            )(current, prec_loc.reshape(nf // B, B), mean_loc.reshape(nf // B, B), fac_loc.T)
 
         sharded = jax.shard_map(
             local_steps,

time: 201 us -> 198 us (0.985)
  local copies, waits for them, and re-layouts: 7.91 us -> 5.36 us
    reshape x2 -> x0, local copies, waits for them, and re-layouts: 2.55 us -> none  [the longest x1 1.28 us: local_steps(): mean_loc.reshape(1, nf)]
where the time goes in v8:
time: 198 us; the launch traced here: 197 us
  Pallas kernels  192 us (97%)
  local copies, waits for them, and re-layouts  5.36 us (3%)
    pallas_call x1, Pallas kernels, local_steps(): pl.pallas_call(functools.partial(kernel, width), out_shape=jax.ShapeDtype...  192 us
    unnamed x1, local copies, waits for them, and re-layouts  5.36 us

profile of v8, /device:TPU:0, one launch (start us, length us, event | category | flops | bytes accessed | tf_op | source)
XLA Modules:
  0.0 197.3 jit_solution(17063007154643511892)
XLA Ops:
  0.0 192.0 %svgd.1 = f32[1536,896]{1,0:T(8,128)} custom-call(f32[1536,896]{1,0:T(8,128)} %x_hbm.1, f32[7,128]{1,0:T(8,128)} %bitcast.4, f32[7,128]{1,0:T(8,128)} %bitcast.5, bf16[16,896]{1,0:T(8,128)(2,1)} %bitcast.3), custom_call_target="tpu_custom_call" | custom-call | tf_op jit(solution)/shard_map/svgd/pallas_call | solution.py:646
  192.0 5.4 %copy.6 = f32[1536,896]{1,0:T(8,128)} copy(f32[1536,896]{1,0:T(8,128)} %svgd.1) | data formatting | bytes 11010048

commit v9 on v8

--- a/solution.py
+++ b/solution.py
@@ -31,6 +31,7 @@
 PM = 6
 DRV0 = AG0 + 3 * LAG2 + PM + 1 + DIE + 1
 ITERS = AG0 + 3 * LAG2 + CH + OUT2 + DIE
+assert YF0 + 10 <= FIN0 and FIN0 + CH <= DRV0 and DRV0 + UP <= ITERS
 
 
 def _ref(k, t, d, ey, c):
@@ -260,8 +261,7 @@
 
         sacc[...] = jnp.zeros_like(sacc)
 
-        @pl.loop(0, ITERS)
-        def _(g):
+        def renew(g):
             gp = jnp.minimum(g, UP - 1)
 
             @pl.when(g < UP)
@@ -295,9 +295,11 @@
             def _():
                 th_copy(_clip(g - 1, UP)).wait()
 
-            @pl.when(g == START + PM)
-            def _():
-                pm_copy().wait()
+        def sums(g, yf):
+            if yf:
+                @pl.when(g == START + PM)
+                def _():
+                    pm_copy().wait()
 
             v = g - YF0
             v_on = (v >= 0) & (v < 2 * rounds)
@@ -305,9 +307,10 @@
             vk = lax.div(v, 2)
             vd = v - 2 * vk
 
-            @pl.when(v_on)
-            def _():
-                gram(gy.at[vd, vk], _ref(vk, 1, vd, 1 - y, c))
+            if yf:
+                @pl.when(v_on)
+                def _():
+                    gram(gy.at[vd, vk], _ref(vk, 1, vd, 1 - y, c))
 
             state = []
             for d in range(2):
@@ -348,11 +351,12 @@
                 def _():
                     gram(gsrc.at[d, i], _ref(k, w, d, e + w * (y - e), c))
 
-                if d == 0:
+                if d == 0 and yf:
                     @pl.when(v_on)
                     def _():
                         y_copy(vd, vk).start()
-                else:
+
+                if d == 1:
                     send_sum(0)
 
                 @pl.when(on)
@@ -376,6 +380,10 @@
                     def _():
                         z_copy(d, i).wait_recv()
                         gsrc[d, i] = gsrc[d, i] + zrecv[d, i]
+
+            if yf:
+                send_sum(1)
+                return
 
             i = g - FIN0
             on = corner & (i >= 0) & (i < chain)
@@ -457,6 +465,7 @@
                     def _():
                         sg_copy(o).start()
 
+        def spread(g):
             heard = []
             for d in range(2):
                 dist = 3 - z if d else z
@@ -547,6 +556,7 @@
                     ke_copy(d, mm, 1 - c).wait_recv()
                     settle(ko.at[1 - c, d, mm], _ref(mm, 1, d, 1 - y, 1 - c))
 
+        def drive(g):
             p = g - DRV0
             on = (p >= 0) & (p < UP)
             p = _clip(p, UP)
@@ -564,6 +574,25 @@
                 cur = theta[panel(p), :]
                 grad = -((cur - mu_ref[0:1, 0:nf]) * lam_ref[0:1, 0:nf] + low)
                 a_ref[panel(p), :] = (grad - rep * cur).astype(bf16)
+
+        @pl.loop(0, UP + 1)
+        def _(g):
+            renew(g)
+            sums(g, True)
+
+        @pl.loop(UP + 1, FIN0)
+        def _(g):
+            sums(g, True)
+
+        @pl.loop(FIN0, FIN0 + CH)
+        def _(g):
+            sums(g, False)
+            spread(g)
+
+        @pl.loop(FIN0 + CH, ITERS)
+        def _(g):
+            spread(g)
+            drive(g)
 
         for e in range(8):
             @pl.when(me != (e // 4) * 12 + e % 4)

time: 198 us -> 193 us (0.975)
  Pallas kernels: 192 us -> 188 us
    pallas_call x1, Pallas kernels: 192 us -> 188 us  [local_steps(): pl.pallas_call(functools.partial(kernel, width), out_shape=jax.ShapeDtype...]
where the time goes in v9:
time: 193 us
  Pallas kernels  188 us (97%)
  local copies, waits for them, and re-layouts  5.36 us (3%)
    pallas_call x1, Pallas kernels, local_steps(): pl.pallas_call(functools.partial(kernel, width), out_shape=jax.ShapeDtype...  188 us
    unnamed x1, local copies, waits for them, and re-layouts  5.36 us

profile of v9, /device:TPU:0, one launch (start us, length us, event | category | flops | bytes accessed | tf_op | source)
XLA Modules:
  0.0 193.3 jit_solution(8241234657270967457)
XLA Ops:
  0.0 187.9 %svgd.1 = f32[1536,896]{1,0:T(8,128)} custom-call(f32[1536,896]{1,0:T(8,128)} %x_hbm.1, f32[7,128]{1,0:T(8,128)} %bitcast.4, f32[7,128]{1,0:T(8,128)} %bitcast.5, bf16[16,896]{1,0:T(8,128)(2,1)} %bitcast.3), custom_call_target="tpu_custom_call" | custom-call | tf_op jit(solution)/shard_map/svgd/pallas_call | solution.py:675
  187.9 5.4 %copy.6 = f32[1536,896]{1,0:T(8,128)} copy(f32[1536,896]{1,0:T(8,128)} %svgd.1) | data formatting | bytes 11010048

commit v10 on v9

--- a/solution.py
+++ b/solution.py
@@ -187,7 +187,7 @@
         def _():
             blk = src[...]
             kf[_span(i), _span(j)] = blk
-            kf[_span(j), _span(i)] = blk.astype(f32).T.astype(bf16)
+            kf[_span(j), _span(i)] = blk.T
 
         @pl.when(e == 1)
         def _():

time: 193 us -> 193 us (level)
  no operation moved by 1% of the time
where the time goes in v10:
time: 193 us
  Pallas kernels  187 us (97%)
  local copies, waits for them, and re-layouts  5.36 us (3%)
    pallas_call x1, Pallas kernels, local_steps(): pl.pallas_call(functools.partial(kernel, width), out_shape=jax.ShapeDtype...  187 us
    unnamed x1, local copies, waits for them, and re-layouts  5.36 us

profile of v10, /device:TPU:0, one launch (start us, length us, event | category | flops | bytes accessed | tf_op | source)
XLA Modules:
  0.0 192.5 jit_solution(6167093075648776608)
XLA Ops:
  0.0 187.1 %svgd.1 = f32[1536,896]{1,0:T(8,128)} custom-call(f32[1536,896]{1,0:T(8,128)} %x_hbm.1, f32[7,128]{1,0:T(8,128)} %bitcast.4, f32[7,128]{1,0:T(8,128)} %bitcast.5, bf16[16,896]{1,0:T(8,128)(2,1)} %bitcast.3), custom_call_target="tpu_custom_call" | custom-call | tf_op jit(solution)/shard_map/svgd/pallas_call | solution.py:675
  187.1 5.4 %copy.6 = f32[1536,896]{1,0:T(8,128)} copy(f32[1536,896]{1,0:T(8,128)} %svgd.1) | data formatting | bytes 11010048

commit v11 on v10

--- a/solution.py
+++ b/solution.py
@@ -19,10 +19,10 @@
 UP = 6
 START = 2
 LAG = 3
-END = 2
+END = 3
 OUT1 = 2
-LAG2 = 3
-OUT2 = 3
+LAG2 = 4
+OUT2 = 5
 DIE = 3
 YF0 = 3
 FIN0 = START + 3 * LAG + END

time: 193 us -> 195 us (1.010)
  Pallas kernels: 187 us -> 190 us
    pallas_call x1, Pallas kernels: 187 us -> 190 us  [local_steps(): pl.pallas_call(functools.partial(kernel, width), out_shape=jax.ShapeDtype...]
where the time goes in v11:
time: 195 us
  Pallas kernels  190 us (97%)
  local copies, waits for them, and re-layouts  5.36 us (3%)
    pallas_call x1, Pallas kernels, local_steps(): pl.pallas_call(functools.partial(kernel, width), out_shape=jax.ShapeDtype...  190 us
    unnamed x1, local copies, waits for them, and re-layouts  5.36 us

profile of v11, /device:TPU:0, one launch (start us, length us, event | category | flops | bytes accessed | tf_op | source)
XLA Modules:
  0.0 195.2 jit_solution(16225779707883088535)
XLA Ops:
  0.0 189.8 %svgd.1 = f32[1536,896]{1,0:T(8,128)} custom-call(f32[1536,896]{1,0:T(8,128)} %x_hbm.1, f32[7,128]{1,0:T(8,128)} %bitcast.4, f32[7,128]{1,0:T(8,128)} %bitcast.5, bf16[16,896]{1,0:T(8,128)(2,1)} %bitcast.3), custom_call_target="tpu_custom_call" | custom-call | tf_op jit(solution)/shard_map/svgd/pallas_call | solution.py:675
  189.8 5.4 %copy.6 = f32[1536,896]{1,0:T(8,128)} copy(f32[1536,896]{1,0:T(8,128)} %svgd.1) | data formatting | bytes 11010048

commit v12 on v10

--- a/solution.py
+++ b/solution.py
@@ -22,8 +22,8 @@
 END = 2
 OUT1 = 2
 LAG2 = 3
-OUT2 = 3
-DIE = 3
+OUT2 = 2
+DIE = 2
 YF0 = 3
 FIN0 = START + 3 * LAG + END
 AG0 = FIN0 + OUT1

time: 193 us -> 196 us (1.016)
  Pallas kernels: 187 us -> 191 us
    pallas_call x1, Pallas kernels: 187 us -> 191 us  [local_steps(): pl.pallas_call(functools.partial(kernel, width), out_shape=jax.ShapeDtype...]
where the time goes in v12:
time: 196 us
  Pallas kernels  191 us (97%)
  local copies, waits for them, and re-layouts  5.36 us (3%)
    pallas_call x1, Pallas kernels, local_steps(): pl.pallas_call(functools.partial(kernel, width), out_shape=jax.ShapeDtype...  191 us
    unnamed x1, local copies, waits for them, and re-layouts  5.36 us

profile of v12, /device:TPU:0, one launch (start us, length us, event | category | flops | bytes accessed | tf_op | source)
XLA Modules:
  0.0 196.3 jit_solution(2332477028417211189)
XLA Ops:
  0.0 190.9 %svgd.1 = f32[1536,896]{1,0:T(8,128)} custom-call(f32[1536,896]{1,0:T(8,128)} %x_hbm.1, f32[7,128]{1,0:T(8,128)} %bitcast.4, f32[7,128]{1,0:T(8,128)} %bitcast.5, bf16[16,896]{1,0:T(8,128)(2,1)} %bitcast.3), custom_call_target="tpu_custom_call" | custom-call | tf_op jit(solution)/shard_map/svgd/pallas_call | solution.py:675
  190.9 5.4 %copy.6 = f32[1536,896]{1,0:T(8,128)} copy(f32[1536,896]{1,0:T(8,128)} %svgd.1) | data formatting | bytes 11010048

commit v13 on v10

--- a/solution.py
+++ b/solution.py
@@ -663,6 +663,21 @@
         out_copy(p).wait()
 
 
+def hand_over(x_hbm, o_hbm, buf, s_in, s_out):
+    n, rows = s_in.shape[0], buf.shape[0] // s_in.shape[0]
+
+    def part(p):
+        return pl.ds(p * rows, rows)
+
+    for p in range(n):
+        pltpu.make_async_copy(x_hbm.at[part(p)], buf.at[part(p)], s_in.at[p]).start()
+    for p in range(n):
+        pltpu.make_async_copy(x_hbm.at[part(p)], buf.at[part(p)], s_in.at[p]).wait()
+        pltpu.make_async_copy(buf.at[part(p)], o_hbm.at[part(p)], s_out.at[p]).start()
+    for p in range(n):
+        pltpu.make_async_copy(buf.at[part(p)], o_hbm.at[part(p)], s_out.at[p]).wait()
+
+
 def solution(mesh):
     def run_steps(particles, prec_diag, mean_vec, low_rank):
         width = particles.shape[1]
@@ -672,7 +687,7 @@
             dma = pltpu.SemaphoreType.DMA
             f32, bf16 = jnp.float32, jnp.bfloat16
             vmem = pltpu.VMEM
-            return pl.pallas_call(
+            res = pl.pallas_call(
                 functools.partial(kernel, width),
                 out_shape=jax.ShapeDtypeStruct((n_part, nf), f32),
                 in_specs=[pl.BlockSpec(memory_space=pl.ANY)] + [pl.BlockSpec(memory_space=pltpu.VMEM)] * 3,
@@ -714,6 +729,14 @@
                 ),
                 name="svgd",
             )(current, prec_loc.reshape(nf // B, B), mean_loc.reshape(nf // B, B), fac_loc.T)
+            return pl.pallas_call(
+                hand_over,
+                out_shape=jax.ShapeDtypeStruct((n_part, nf), f32),
+                in_specs=[pl.BlockSpec(memory_space=pl.ANY)],
+                out_specs=pl.BlockSpec(memory_space=pl.ANY),
+                scratch_shapes=[vmem((n_part, nf), f32), dma((16,)), dma((16,))],
+                name="hand_over",
+            )(res)
 
         sharded = jax.shard_map(
             local_steps,

time: 193 us -> 192 us (level)
  local copies, waits for them, and re-layouts: 5.36 us -> 0 us
  Pallas kernels: 187 us -> 192 us
    unnamed x1 -> x0, local copies, waits for them, and re-layouts: 5.36 us -> none
    pallas_call x0 -> x1, Pallas kernels: none -> 5.11 us  [local_steps(): pl.pallas_call(hand_over, out_shape=jax.ShapeDtypeStruct((n_part, nf), f3...]
where the time goes in v13:
time: 192 us
  Pallas kernels  192 us (100%)
    pallas_call x1, Pallas kernels, local_steps(): pl.pallas_call(functools.partial(kernel, width), out_shape=jax.ShapeDtype...  187 us
    pallas_call x1, Pallas kernels, local_steps(): pl.pallas_call(hand_over, out_shape=jax.ShapeDtypeStruct((n_part, nf), f3...  5.11 us

profile of v13, /device:TPU:0, one launch (start us, length us, event | category | flops | bytes accessed | tf_op | source)
XLA Modules:
  0.0 192.3 jit_solution(5232079510572984864)
XLA Ops:
  0.0 187.1 %svgd.1.x_hbm = f32[1536,896]{1,0:T(8,128)} custom-call(f32[1536,896]{1,0:T(8,128)} %x_hbm.1, f32[7,128]{1,0:T(8,128)} %bitcast.4, f32[7,128]{1,0:T(8,128)} %bitcast.5, bf16[16,896]{1,0:T(8,128)(2,1)} %bitcast.3), custom_call_target="tpu_custom_call" | custom-call | tf_op jit(solution)/shard_map/svgd/pallas_call | solution.py:690
  187.1 5.1 %hand_over.1 = f32[1536,896]{1,0:T(8,128)} custom-call(f32[1536,896]{1,0:T(8,128)} %svgd.1.x_hbm), custom_call_target="tpu_custom_call" | custom-call | tf_op jit(solution)/shard_map/hand_over/pallas_call | solution.py:732

commit v14 on v10

--- a/solution.py
+++ b/solution.py
@@ -55,9 +55,9 @@
     return pl.ds(pl.multiple_of(i * B, B), B)
 
 
-def kernel(width, x_hbm, lam_in, mu_in, ut_ref, o_hbm, theta, th, a_ref, kf, kc, ko, gsrc, gy, zrecv, yrecv, yend, pmb, pmrecv,
+def kernel(width, x_hbm, lam_in, mu_in, ut_ref, theta, th, a_ref, kf, kc, ko, gsrc, gy, zrecv, yrecv, yend, pmb, pmrecv,
            ps, pzr, pye, pmf, lam_ref, mu_ref,
-           dsrc, dgather, dsum, sacc, sgather, ssum, ld, od, thd_s, thd_r, pm_s, pm_r, dg_s, dg_r, sg_s, sg_r,
+           dsrc, dgather, dsum, sacc, sgather, ssum, ld, thd_s, thd_r, pm_s, pm_r, dg_s, dg_r, sg_s, sg_r,
            zs, zr, ys, yr, ye_s, ye_r, kz_s, kz_r, kyz_s, kyz_r, ky_s, ky_r, kd_s, kd_r, ke_s, ke_r,
            pz_s, pz_r, pye_s, pye_r, pky_s, pky_r, pkz_s, pkz_r, pkd_s, pkd_r):
     nf = theta.shape[1]
@@ -103,9 +103,6 @@
     def load_copy(p):
         return pltpu.make_async_copy(x_hbm.at[panel(p)], theta.at[panel(p)], ld.at[p])
 
-    def out_copy(p):
-        return pltpu.make_async_copy(theta.at[panel(p)], o_hbm.at[panel(p)], od.at[p])
-
     def th_copy(p):
         return rcopy(th.at[panel(p), pl.ds(0, nf)], th.at[panel(p), pl.ds(nf, nf)], thd_s.at[p], thd_r.at[p], dpart)
 
@@ -656,11 +653,6 @@
     @pl.loop(0, UP)
     def _(p):
         update(p)
-        out_copy(p).start()
-
-    @pl.loop(0, UP)
-    def _(p):
-        out_copy(p).wait()
 
 
 def solution(mesh):
@@ -672,13 +664,12 @@
             dma = pltpu.SemaphoreType.DMA
             f32, bf16 = jnp.float32, jnp.bfloat16
             vmem = pltpu.VMEM
-            return pl.pallas_call(
+            res = pl.pallas_call(
                 functools.partial(kernel, width),
-                out_shape=jax.ShapeDtypeStruct((n_part, nf), f32),
+                out_shape=pltpu.VMEM((n_part, nf), f32),
                 in_specs=[pl.BlockSpec(memory_space=pl.ANY)] + [pl.BlockSpec(memory_space=pltpu.VMEM)] * 3,
-                out_specs=pl.BlockSpec(memory_space=pl.ANY),
+                out_specs=pl.BlockSpec(memory_space=pltpu.VMEM),
                 scratch_shapes=[
-                    vmem((n_part, nf), f32),
                     vmem((n_part, 2 * nf), bf16),
                     vmem((n_part, nf), bf16),
                     vmem((n_part, n_part), bf16),
@@ -703,7 +694,7 @@
                     vmem((16, B), f32),
                     vmem((8, 16, B), f32),
                     vmem((16, B), f32),
-                    dma((UP,)), dma((UP,)), dma((UP,)), dma((UP,)), dma, dma, dma((8,)), dma((16,)), dma((16,)), dma((8,)),
+                    dma((UP,)), dma((UP,)), dma((UP,)), dma, dma, dma((8,)), dma((16,)), dma((16,)), dma((8,)),
                     dma((2, CH)), dma((2, CH)), dma((2, 5)), dma((2, 5)), dma((5,)), dma((5,)),
                     dma((2, CH)), dma((2, CH)), dma((5,)), dma((5,)), dma((2, 5)), dma((2, 5)),
                     dma((2, CH)), dma((2, CH)), dma((2, 5)), dma((2, 5)),
@@ -714,6 +705,7 @@
                 ),
                 name="svgd",
             )(current, prec_loc.reshape(nf // B, B), mean_loc.reshape(nf // B, B), fac_loc.T)
+            return res
 
         sharded = jax.shard_map(
             local_steps,

time: 193 us -> 189 us (0.979)
  local copies, waits for them, and re-layouts: 5.36 us -> 2.45 us
    unnamed x1, local copies, waits for them, and re-layouts: 5.36 us -> 2.45 us
where the time goes in v14:
time: 189 us; the launch traced here: 188 us
  Pallas kernels  186 us (98%)
  local copies, waits for them, and re-layouts  2.45 us (1%)
    pallas_call x1, Pallas kernels, local_steps(): pl.pallas_call(functools.partial(kernel, width), out_shape=pltpu.VMEM((n_...  186 us

profile of v14, /device:TPU:0, one launch (start us, length us, event | category | flops | bytes accessed | tf_op | source)
XLA Modules:
  0.0 188.4 jit_solution(18356441247150005873)
XLA Ops:
  0.0 185.9 %svgd.1 = f32[1536,896]{1,0:T(8,128)S(1)} custom-call(f32[1536,896]{1,0:T(8,128)} %x_hbm.1, f32[7,128]{1,0:T(8,128)} %bitcast.4, f32[7,128]{1,0:T(8,128)} %bitcast.5, bf16[16,896]{1,0:T(8,128)(2,1)} %bitcast.3), custom_call_target="tpu_custom_call" | custom-call | tf_op jit(solution)/shard_map/svgd/pallas_call | solution.py:667
  186.0 2.4 %copy.6 = f32[1536,896]{1,0:T(8,128)} copy(f32[1536,896]{1,0:T(8,128)S(1)} %svgd.1) | data formatting | bytes 11010048
